TPU v7x, 256 devices: a whole 4x4x8 slice. The times are simulated.
256 devices in a mesh: dp: 64 (over z, y_lo, x), tensor: 4 (over y_hi, core).
Axes of the slice: x: 4, y: 4 (y_hi: 2, y_lo: 2; y = y_hi * 2 + y_lo), z: 8, core: 2. Of those that a mesh axis runs over, the one named last changes fastest.
Arguments:
- out_first: bfloat16 [64, 197, 1024], P('dp', None, 'tensor'), may hold values from -6 to 6
- out_second: bfloat16 [64, 197, 1024], P('dp', None, 'tensor'), may hold values from -6 to 6
- grad_first: bfloat16 [64, 197, 1024], P('dp', None, 'tensor'), may hold values from -6 to 6
- grad_second: bfloat16 [64, 197, 1024], P('dp', None, 'tensor'), may hold values from -16 to 16
- gain_attn: float32 [1024], replicated, may hold values from 0.25 to 1.75
- gain_mlp: float32 [1024], replicated, may hold values from 0.25 to 1.75
- qkv_weight: bfloat16 [1024, 3, 1024], P(None, None, 'tensor'), may hold values from -1 to 1
- proj_weight: bfloat16 [1024, 1024], P(None, 'tensor'), may hold values from -0.1875 to 0.1875
- inner_weight: bfloat16 [1024, 4096], P(None, 'tensor'), may hold values from -0.1875 to 0.1875
- inner_bias: float32 [4096], P('tensor'), may hold values from -3 to 3
- outer_weight: bfloat16 [1024, 4096], P(None, 'tensor'), may hold values from -0.09375 to 0.09375
Outputs:
- input_first: bfloat16 [64, 197, 1024], P('dp', None, 'tensor')
- input_second: bfloat16 [64, 197, 1024], P('dp', None, 'tensor')
- back_first: bfloat16 [64, 197, 1024], P('dp', None, 'tensor')
- back_second: bfloat16 [64, 197, 1024], P('dp', None, 'tensor')
- grad_qkv: float32 [1024, 3, 1024], P('dp', None, 'tensor')
- grad_proj: float32 [1024, 1024], P('dp', 'tensor')
- grad_inner: float32 [1024, 4096], P('dp', 'tensor')
- grad_bias: float32 [4096], P('tensor')
- grad_outer: float32 [1024, 4096], P('dp', 'tensor')
- grad_gain_attn: float32 [1024], P('tensor')
- grad_gain_mlp: float32 [1024], P('tensor')
All inputs are finite; a program needn't handle non-finite values.
Results may differ from a plain program's by a relative error of at most 0.016.
Values may be sent and summed in bfloat16 or wider, within the bound.
A program may use at most 64 MiB of HBM per device.

v0:
```python
import jax
import jax.numpy as jnp
from jax import lax
from jax.sharding import Mesh
from jax.sharding import PartitionSpec as P

D = 1024
HEADS = 16
DP = ("dp_0", "dp_1", "dp_2")


epsilon = 1e-06


def split_up(x, dim, devices):
    dims = x.shape
    pieces = x.reshape(*dims[:dim], devices, dims[dim] // devices, *dims[dim + 1 :])
    return jnp.moveaxis(pieces, dim, 0)


def summed_on_arrival(x, axis, dim):
    pieces = split_up(x, dim, lax.axis_size(axis))
    arrived = lax.all_to_all(pieces, axis, split_axis=0, concat_axis=0, tiled=True)
    return arrived.astype(jnp.float32).sum(axis=0)


def sent_to_all(x, axis):
    copies = jnp.broadcast_to(x, (lax.axis_size(axis), *x.shape))
    return lax.all_to_all(copies, axis, split_axis=0, concat_axis=0, tiled=True)


def of_everyone(x, axis):
    everything = sent_to_all(x, axis)
    return jnp.sum(everything, axis=0)


def packed_total(arrays, axis):
    flat, at, finished = (jnp.concatenate([a.reshape(-1) for a in arrays]), 0, [])
    subtotal = of_everyone(flat, axis)
    for a in arrays:
        finished.append(subtotal[at : at + a.size].reshape(a.shape))
        at += a.size
    return tuple(finished)


def side_by_side(arrays, axis, dim, along):
    widths = [a.shape[along] for a in arrays]
    both = jnp.concatenate(arrays, axis=along)
    whole = lax.all_gather(both, axis, axis=dim, tiled=True)
    return tuple(jnp.split(whole, [sum(widths[:k]) for k in range(1, len(widths))], axis=along))


def summed_on_arrival_2(x, axis, dim):
    devices = lax.axis_size(axis)
    pieces = lax.all_to_all(split_up(x, dim, devices), axis, 0, 0, tiled=True)
    return jnp.sum(pieces, axis=0)


def sum_in_order(pieces, axes, order):
    inside = pieces.shape[1:]
    pieces = pieces.reshape(*(lax.axis_size(a) for a in axes), *inside)
    pieces = jnp.moveaxis(pieces, order, range(len(axes))).reshape(-1, *inside)
    for k in order:
        pieces = lax.psum_scatter(pieces, axes[k], scatter_dimension=0, tiled=True)
    return pieces[0]


def scatter_axes(x, axes, order, dim):
    devices = lax.axis_size(axes)
    return sum_in_order(split_up(x, dim, devices), axes, order)


def normalize(values):
    centre = values - jnp.mean(values, -1, keepdims=True)
    spread = lax.rsqrt(jnp.mean(centre * centre, -1, keepdims=True) + epsilon)
    return (centre * spread, spread)


def weight_term(left_rows, right_rows):
    return lax.dot_general(
        left_rows, right_rows, (((0,), (0,)), ((), ())), preferred_element_type=jnp.float32
    )


def norm_backward(grad_part, normed, spread, gain, offset, local_width):
    full_width = normed.shape[1]
    own_part = summed_on_arrival(grad_part.astype(jnp.bfloat16), "tensor", 1)
    own_normed = lax.dynamic_slice_in_dim(normed, offset, local_width, 1)
    own_gain = lax.dynamic_slice_in_dim(gain, offset, local_width, 0)
    scaled = own_part * own_gain
    totals = packed_total((jnp.sum(scaled, 1), jnp.sum(scaled * own_normed, 1)), "tensor")
    first_mean = totals[0][:, None] / full_width
    second_mean = totals[1][:, None] / full_width
    back_rows = spread * (scaled - first_mean - own_normed * second_mean)
    return (back_rows, jnp.sum(own_part * own_normed, 0))


def on_device(
    out_first,
    out_second,
    grad_first,
    grad_second,
    gain_attn,
    gain_mlp,
    qkv_weight,
    proj_weight,
    inner_weight,
    inner_bias,
    outer_weight,
):
    images, length, local_width = out_first.shape
    full_width = local_width * lax.axis_size("tensor")
    rows_all = images * length
    head_dim = D // HEADS
    local_heads = local_width // head_dim
    factor = head_dim ** (-0.5)
    shard_rows = full_width // lax.axis_size(DP)
    offset = lax.axis_index("tensor") * local_width
    hidden_width = inner_weight.shape[1]
    whole_first, whole_lower = side_by_side((out_first, grad_second), "tensor", 2, 0)
    first_rows = whole_first.reshape(rows_all, full_width).astype(jnp.float32)
    lower_grad = whole_lower.reshape(rows_all, full_width)
    normed_mlp, spread_mlp = normalize(first_rows)
    input_mlp = (normed_mlp * gain_mlp).astype(jnp.bfloat16)
    hidden = jnp.dot(input_mlp, inner_weight, preferred_element_type=jnp.float32) + inner_bias
    active = jax.nn.gelu(hidden).astype(jnp.bfloat16)
    mlp_part = summed_on_arrival_2(
        jnp.dot(active, outer_weight.T, preferred_element_type=jnp.float32), "tensor", 1
    )
    input_second = (
        out_second.reshape(rows_all, local_width).astype(jnp.float32) - mlp_part
    ).astype(jnp.bfloat16)
    grad_active = jnp.dot(lower_grad, outer_weight, preferred_element_type=jnp.float32)
    grad_hidden = jax.vjp(jax.nn.gelu, hidden)[1](grad_active)[0].astype(jnp.bfloat16)
    bias_part = jnp.sum(grad_hidden.astype(jnp.float32), 0)
    grad_norm_mlp = jnp.dot(grad_hidden, inner_weight.T, preferred_element_type=jnp.float32)
    back_mlp, gain_mlp_part = norm_backward(
        grad_norm_mlp, normed_mlp, spread_mlp, gain_mlp, offset, local_width
    )
    back_first = (grad_first.reshape(rows_all, local_width).astype(jnp.float32) + back_mlp).astype(
        jnp.bfloat16
    )
    whole_second, whole_back = side_by_side(
        (
            input_second.reshape(images, length, local_width),
            back_first.reshape(images, length, local_width),
        ),
        "tensor",
        2,
        0,
    )
    normed_attn, spread_attn = normalize(
        whole_second.reshape(rows_all, full_width).astype(jnp.float32)
    )
    input_attn = (normed_attn * gain_attn).astype(jnp.bfloat16)
    back_rows_all = whole_back.reshape(rows_all, full_width)
    qkv_rows = jnp.einsum(
        "td,dcj->tcj", input_attn, qkv_weight, preferred_element_type=jnp.float32
    ).astype(jnp.bfloat16)
    shaped = qkv_rows.reshape(images, length, 3, local_heads, head_dim)
    queries = shaped[:, :, 0]
    key_rows = shaped[:, :, 1]
    value_rows = shaped[:, :, 2]
    grad_heads = (
        jnp.dot(back_rows_all, proj_weight, preferred_element_type=jnp.float32)
        .astype(jnp.bfloat16)
        .reshape(images, length, local_heads, head_dim)
    )
    scores = (
        jnp.einsum("bqhe,bkhe->bhqk", queries, key_rows, preferred_element_type=jnp.float32)
        * factor
    )
    attn_probs = jax.nn.softmax(scores, -1)
    probs_low = attn_probs.astype(jnp.bfloat16)
    heads_out = jnp.einsum(
        "bhqk,bkhe->bqhe", probs_low, value_rows, preferred_element_type=jnp.float32
    ).astype(jnp.bfloat16)
    grad_probs = jnp.einsum(
        "bqhe,bkhe->bhqk", grad_heads, value_rows, preferred_element_type=jnp.float32
    )
    grad_value = jnp.einsum(
        "bhqk,bqhe->bkhe", probs_low, grad_heads, preferred_element_type=jnp.float32
    ).astype(jnp.bfloat16)
    row_dot = jnp.sum(grad_probs * attn_probs, -1, keepdims=True)
    grad_scores = (attn_probs * (grad_probs - row_dot)).astype(jnp.bfloat16)
    grad_query = (
        jnp.einsum("bhqk,bkhe->bqhe", grad_scores, key_rows, preferred_element_type=jnp.float32)
        * factor
    ).astype(jnp.bfloat16)
    grad_key = (
        jnp.einsum("bhqk,bqhe->bkhe", grad_scores, queries, preferred_element_type=jnp.float32)
        * factor
    ).astype(jnp.bfloat16)
    grad_rows = jnp.stack([grad_query, grad_key, grad_value], 2).reshape(rows_all, 3 * local_width)
    attn_rows = heads_out.reshape(rows_all, local_width)
    attn_part = summed_on_arrival(
        jnp.dot(attn_rows, proj_weight.T, preferred_element_type=jnp.float32).astype(jnp.bfloat16),
        "tensor",
        1,
    )
    input_first = (out_first.reshape(rows_all, local_width).astype(jnp.float32) - attn_part).astype(
        jnp.bfloat16
    )
    flat_qkv = qkv_weight.reshape(full_width, 3 * local_width)
    grad_norm_attn = jnp.dot(grad_rows, flat_qkv.T, preferred_element_type=jnp.float32)
    back_attn, gain_attn_part = norm_backward(
        grad_norm_attn, normed_attn, spread_attn, gain_attn, offset, local_width
    )
    back_second = (
        grad_second.reshape(rows_all, local_width).astype(jnp.float32) + back_attn
    ).astype(jnp.bfloat16)
    joined = scatter_axes(
        jnp.concatenate(
            [
                weight_term(input_attn, grad_rows),
                weight_term(back_rows_all, attn_rows),
                weight_term(input_mlp, grad_hidden),
                weight_term(lower_grad, active),
            ],
            1,
        ).astype(jnp.bfloat16),
        DP,
        (0, 2, 1),
        0,
    ).astype(jnp.float32)
    grad_qkv = joined[:, : 3 * local_width]
    grad_proj = joined[:, 3 * local_width : 4 * local_width]
    grad_inner = joined[:, 4 * local_width : 4 * local_width + hidden_width]
    grad_outer = joined[:, 4 * local_width + hidden_width :]
    summed_small = packed_total((gain_attn_part, gain_mlp_part, bias_part), DP)
    shape_out = (images, length, local_width)
    return (
        input_first.reshape(shape_out),
        input_second.reshape(shape_out),
        back_first.reshape(shape_out),
        back_second.reshape(shape_out),
        grad_qkv.reshape(shard_rows, 3, local_width),
        grad_proj,
        grad_inner,
        summed_small[2],
        grad_outer,
        summed_small[0],
        summed_small[1],
    )


def solution(mesh):
    split = Mesh(
        mesh.devices.reshape(8, 2, 4, mesh.shape["tensor"]), ("dp_0", "dp_1", "dp_2", "tensor")
    )
    return jax.shard_map(
        on_device,
        mesh=split,
        in_specs=(
            P(DP, None, "tensor"),
            P(DP, None, "tensor"),
            P(DP, None, "tensor"),
            P(DP, None, "tensor"),
            P(),
            P(),
            P(None, None, "tensor"),
            P(None, "tensor"),
            P(None, "tensor"),
            P("tensor"),
            P(None, "tensor"),
        ),
        out_specs=(
            P(DP, None, "tensor"),
            P(DP, None, "tensor"),
            P(DP, None, "tensor"),
            P(DP, None, "tensor"),
            P(DP, None, "tensor"),
            P(DP, "tensor"),
            P(DP, "tensor"),
            P("tensor"),
            P(DP, "tensor"),
            P("tensor"),
            P("tensor"),
        ),
        check_vma=False,
    )
```

profile of v0, /device:TPU:2, one launch (start us, length us, event | category | flops | bytes accessed | tf_op | source)
XLA Modules:
  0.0 251.6 jit_solution(8271185419312058462)
XLA Ops:
  8.3 10.6 %all_gather.6 = bf16[2,197,1024]{2,1,0:T(8,128)(2,1)S(1)} all-gather(bf16[2,197,256]{2,1,0:T(8,128)(2,1)S(1)} %pad_maximum_fusion.1), channel_id=1, replica_groups=mesh['dp_0'=8,'dp_1'=2,'dp_2'=4,'tensor'=4] {'tensor'}, dimensions={2}, use_global_device_ids=true | all-gather | bytes 1008640 | tf_op jit(solution)/shard_map/all_gather | solution.py:49
  20.1 1.6 convert_reduce_fusion.2
  24.3 1.8 copy.158
  26.1 4.1 %all-to-all-start.1 = ((bf16[4,197,256]{2,1,0:T(8,128)(2,1)}), bf16[4,197,256]{2,1,0:T(8,128)(2,1)}, u32[]{:S(2)}, u32[]{:S(2)}) async-start(bf16[4,197,256]{2,1,0:T(8,128)(2,1)} %bitcast.199), calls=%async_computation.1 | async-start | bytes 819200 | tf_op jit(solution)/shard_map/all_to_all | solution.py:23
  31.9 2.9 %fusion.51 = f32[197,1024]{1,0:T(8,128)} fusion(bf16[1024,1024]{1,0:T(8,128)(2,1)S(1)} %copy-done, f32[197,1024]{1,0:T(8,128)} %copy-done.21), kind=kOutput, calls=%fused_computation.116 | convolution fusion | flops 414954496 | bytes 3710976 | tf_op jit(solution)/shard_map/dot_general | solution.py:128
  34.8 4.6 %all-to-all-done.1 = bf16[4,197,256]{2,1,0:T(8,128)(2,1)} async-done(((bf16[4,197,256]{2,1,0:T(8,128)(2,1)}), bf16[4,197,256]{2,1,0:T(8,128)(2,1)}, u32[]{:S(2)}, u32[]{:S(2)}) %all-to-all-start.1) | async-done | bytes 403488 | tf_op jit(solution)/shard_map/all_to_all | solution.py:23
  41.2 1.7 multiply_reduce_fusion.1
  43.5 3.2 %all-to-all-start.2 = ((f32[4,1,394]{2,1,0:T(1,128)}), f32[4,1,394]{2,1,0:T(1,128)S(1)}, u32[]{:S(2)}, u32[]{:S(2)}) async-start(f32[4,1,394]{2,1,0:T(1,128)} %broadcast_in_dim.6), calls=%async_computation.2 | async-start | bytes 16384 | tf_op jit(solution)/shard_map/all_to_all | solution.py:29
  46.8 3.3 %convolution_convert_fusion = bf16[8,2,4,16,1024]{4,3,2,1,0:T(8,128)(2,1)} fusion(bf16[8,2,4,16,197]{4,3,2,1,0:T(8,128)(2,1)S(1)} %bitcast.216, f32[197,1024]{1,0:T(8,128)} %copy-done.21), kind=kOutput, calls=%fused_computation.2 | convolution fusion | flops 416003072 | bytes 3307520 | tf_op jit(solution)/shard_map/dot_general | solution.py:80
  53.9 4.8 %all-to-all-start = ((f32[4,197,256]{2,1,0:T(8,128)}), f32[4,197,256]{2,1,0:T(8,128)S(1)}, u32[]{:S(2)}, u32[]{:S(2)}) async-start(f32[4,197,256]{2,1,0:T(8,128)} %bitcast.196), calls=%async_computation | async-start | bytes 1638400 | tf_op jit(solution)/shard_map/all_to_all | solution.py:55
  58.7 3.0 %convolution_convert_fusion.1 = bf16[8,2,4,16,1024]{4,3,2,1,0:T(8,128)(2,1)} fusion(bf16[8,2,4,16,197]{4,3,2,1,0:T(8,128)(2,1)S(1)} %bitcast.207, bf16[197,1024]{1,0:T(8,128)(2,1)} %copy-done.5), kind=kOutput, calls=%fused_computation.3 | convolution fusion | flops 414187520 | bytes 2904064 | tf_op jit(solution)/shard_map/dot_general | solution.py:80
  63.1 9.1 %all-to-all-done = f32[4,197,256]{2,1,0:T(8,128)S(1)} async-done(((f32[4,197,256]{2,1,0:T(8,128)}), f32[4,197,256]{2,1,0:T(8,128)S(1)}, u32[]{:S(2)}, u32[]{:S(2)}) %all-to-all-start) | async-done | bytes 806944 | tf_op jit(solution)/shard_map/all_to_all | solution.py:55
  72.9 9.8 %all_gather.7 = bf16[2,197,1024]{2,1,0:T(8,128)(2,1)S(1)} all-gather(bf16[2,197,256]{2,1,0:T(8,128)(2,1)S(1)} %pad_maximum_fusion.2), channel_id=1, replica_groups=mesh['dp_0'=8,'dp_1'=2,'dp_2'=4,'tensor'=4] {'tensor'}, dimensions={2}, use_global_device_ids=true | all-gather | bytes 1008640 | tf_op jit(solution)/shard_map/all_gather | solution.py:49
  90.9 1.5 multiply_reduce_fusion
  97.4 2.0 copy.117
  102.5 2.6 %maximum_bitcast_fusion = bf16[8,4,2,16,3072]{4,3,1,2,0:T(8,128)(2,1)S(1)} fusion(bf16[8,2,4,16,1024]{4,3,2,1,0:T(8,128)(2,1)} %convolution_convert_fusion, bf16[8,2,4,16,1024]{4,3,2,1,0:T(8,128)(2,1)S(1)} %copy-done.1, bf16[8,2,4,16,256]{4,3,2,1,0:T(8,128)(2,1)S(1)} %convolution_convert_fusion.3, bf16[8,2,4,16,768]{4,3,2,1,0:T(8,128)(2,1)S(1)} %convolution_convert_fusion.2), kind=kLoop, calls=%fused_computation.1 | loop fusion | flops 25165824 | bytes 12582912 | tf_op jit(solution)/shard_map/transpose | solution.py:62
  105.1 3.1 %copy.123 = bf16[8,4,2,16,3072]{4,3,2,1,0:T(8,128)(2,1)} copy(bf16[8,4,2,16,3072]{4,3,1,2,0:T(8,128)(2,1)S(1)} %maximum_bitcast_fusion) | data formatting | bytes 12582912 | tf_op jit(solution)/shard_map/transpose | solution.py:62
  108.3 2.6 %copy.113 = bf16[1024,3,256]{0,2,1:T(8,128)(2,1)} copy(bf16[1024,3,256]{2,0,1:T(8,128)(2,1)} %param.17) | data formatting | bytes 3145728 | tf_op args[6]
  110.9 2.7 %convolution_convert_fusion.4 = bf16[197,1024]{1,0:T(8,128)(2,1)} fusion(bf16[197,768]{0,1:T(8,128)(2,1)S(1)} %bitcast.204, bf16[1024,768]{0,1:T(8,128)(2,1)} %bitcast.202), kind=kOutput, calls=%fused_computation.10 | convolution fusion | flops 310055936 | bytes 2278912 | tf_op jit(solution)/shard_map/dot_general | solution.py:205
  115.7 3.5 %all-to-all-start.4 = ((bf16[4,197,256]{2,1,0:T(8,128)(2,1)}), bf16[4,197,256]{2,1,0:T(8,128)(2,1)S(1)}, u32[]{:S(2)}, u32[]{:S(2)}) async-start(bf16[4,197,256]{2,1,0:T(8,128)(2,1)} %bitcast.208), calls=%async_computation.4 | async-start | bytes 819200 | tf_op jit(solution)/shard_map/all_to_all | solution.py:23
  119.2 65.5 %reduce-scatter.4.cloned.1.call-done = bf16[8,16,3072]{2,1,0:T(8,128)(2,1)} async-done(((bf16[64,16,3072]{2,1,0:T(8,128)(2,1)}), bf16[8,16,3072]{2,1,0:T(8,128)(2,1)}) %reduce-scatter.4.cloned.1.call-update) | async-done | bytes 786448 | tf_op jit(solution)/shard_map/reduce_scatter | solution.py:64
  184.7 2.2 convolution_convert_fusion.6
  186.9 2.0 reshape.241
  188.8 1.8 copy.157
  191.8 4.4 %all-to-all-start.3 = ((bf16[4,197,256]{2,1,0:T(8,128)(2,1)}), bf16[4,197,256]{2,1,0:T(8,128)(2,1)S(1)}, u32[]{:S(2)}, u32[]{:S(2)}) async-start(bf16[4,197,256]{2,1,0:T(8,128)(2,1)} %bitcast.209), calls=%async_computation.3 | async-start | bytes 819200 | tf_op jit(solution)/shard_map/all_to_all | solution.py:23
  197.4 7.8 %all-to-all-done.3 = bf16[4,197,256]{2,1,0:T(8,128)(2,1)S(1)} async-done(((bf16[4,197,256]{2,1,0:T(8,128)(2,1)}), bf16[4,197,256]{2,1,0:T(8,128)(2,1)S(1)}, u32[]{:S(2)}, u32[]{:S(2)}) %all-to-all-start.3) | async-done | bytes 403488 | tf_op jit(solution)/shard_map/all_to_all | solution.py:23
  205.9 3.2 %all-to-all-start.5 = ((f32[4,1,394]{2,1,0:T(1,128)}), f32[4,1,394]{2,1,0:T(1,128)S(1)}, u32[]{:S(2)}, u32[]{:S(2)}) async-start(f32[4,1,394]{2,1,0:T(1,128)} %broadcast_in_dim.7), calls=%async_computation.5 | async-start | bytes 16384 | tf_op jit(solution)/shard_map/all_to_all | solution.py:29
  209.2 5.2 %all-to-all-done.5 = f32[4,1,394]{2,1,0:T(1,128)S(1)} async-done(((f32[4,1,394]{2,1,0:T(1,128)}), f32[4,1,394]{2,1,0:T(1,128)S(1)}, u32[]{:S(2)}, u32[]{:S(2)}) %all-to-all-start.5) | async-done | bytes 6336 | tf_op jit(solution)/shard_map/all_to_all | solution.py:29
  215.4 8.0 %all-to-all-start.6 = ((f32[64,1,1536]{2,1,0:T(1,128)}), f32[64,1,1536]{2,1,0:T(1,128)S(1)}, u32[]{:S(2)}, u32[]{:S(2)}) async-start(f32[64,1,1536]{2,1,0:T(1,128)} %broadcast_in_dim.8), calls=%async_computation.9 | async-start | bytes 786432 | tf_op jit(solution)/shard_map/all_to_all | solution.py:29
  224.3 1.7 fusion.48
  226.0 11.9 %all-to-all-done.6 = f32[64,1,1536]{2,1,0:T(1,128)S(1)} async-done(((f32[64,1,1536]{2,1,0:T(1,128)}), f32[64,1,1536]{2,1,0:T(1,128)S(1)}, u32[]{:S(2)}, u32[]{:S(2)}) %all-to-all-start.6) | async-done | bytes 393248 | tf_op jit(solution)/shard_map/all_to_all | solution.py:29
  239.3 3.0 %reduce-scatter.8.cloned.1.call-done = bf16[1,16,3072]{2,1,0:T(8,128)(2,1)} async-done(((bf16[2,16,3072]{2,1,0:T(8,128)(2,1)}), bf16[1,16,3072]{2,1,0:T(8,128)(2,1)}) %reduce-scatter.8.cloned.1.call-update) | async-done | bytes 98320 | tf_op jit(solution)/shard_map/reduce_scatter | solution.py:64
  (119 shorter events, 42.2 us)
Async XLA Ops:
  7.2 13.0 %copy-start = (bf16[1024,1024]{1,0:T(8,128)(2,1)S(1)}, bf16[1024,1024]{1,0:T(8,128)(2,1)}, u32[]{:S(2)}) copy-start(bf16[1024,1024]{1,0:T(8,128)(2,1)} %param.21) | copy-start | bytes 6291460
  7.2 12.2 %copy-start.15 = (f32[1024]{0:T(1024)S(1)}, f32[1024]{0:T(1024)}, u32[]{:S(2)}) copy-start(f32[1024]{0:T(1024)} %param.16) | copy-start | bytes 12292
  7.2 12.2 %copy-start.3 = (bf16[1024,1024]{1,0:T(8,128)(2,1)S(1)}, bf16[1024,1024]{1,0:T(8,128)(2,1)}, u32[]{:S(2)}) copy-start(bf16[1024,1024]{1,0:T(8,128)(2,1)} %param.19) | copy-start | bytes 6291460
  7.2 12.2 %copy-start.20 = (f32[1024]{0:T(1024)S(1)}, f32[1024]{0:T(1024)}, u32[]{:S(2)}) copy-start(f32[1024]{0:T(1024)} %param.20) | copy-start | bytes 12292
  20.1 1.6 copy-start.21
  21.7 0.8 copy-start.5
  26.1 13.3 %all-to-all-start.1 = ((bf16[4,197,256]{2,1,0:T(8,128)(2,1)}), bf16[4,197,256]{2,1,0:T(8,128)(2,1)}, u32[]{:S(2)}, u32[]{:S(2)}) async-start(bf16[4,197,256]{2,1,0:T(8,128)(2,1)} %bitcast.199), calls=%async_computation.1 | async-start | bytes 819200 | tf_op jit(solution)/shard_map/all_to_all | solution.py:23
  31.7 8.8 %copy-start.14 = (f32[256]{0:T(256)}, f32[256]{0:T(256)S(1)}, u32[]{:S(2)}) copy-start(f32[256]{0:T(256)S(1)} %dynamic_slice.12) | copy-start | bytes 3076
  40.5 0.7 copy-start.4
  43.5 10.4 %all-to-all-start.2 = ((f32[4,1,394]{2,1,0:T(1,128)}), f32[4,1,394]{2,1,0:T(1,128)S(1)}, u32[]{:S(2)}, u32[]{:S(2)}) async-start(f32[4,1,394]{2,1,0:T(1,128)} %broadcast_in_dim.6), calls=%async_computation.2 | async-start | bytes 16384 | tf_op jit(solution)/shard_map/all_to_all | solution.py:29
  53.9 18.2 %all-to-all-start = ((f32[4,197,256]{2,1,0:T(8,128)}), f32[4,197,256]{2,1,0:T(8,128)S(1)}, u32[]{:S(2)}, u32[]{:S(2)}) async-start(f32[4,197,256]{2,1,0:T(8,128)} %bitcast.196), calls=%async_computation | async-start | bytes 1638400 | tf_op jit(solution)/shard_map/all_to_all | solution.py:55
  58.7 126.0 %reduce-scatter.4.cloned.1.call-start = ((), (), s32[]{:S(2)}) async-start(), calls=%async_computation.10 | async-start | bytes 7077888 | tf_op jit(solution)/shard_map/reduce_scatter | solution.py:64
  58.7 13.5 %copy-start.13 = (bf16[1,197,256]{2,1,0:T(8,128)(2,1)S(1)}, bf16[1,197,256]{2,1,0:T(8,128)(2,1)}, u32[]{:S(2)}) copy-start(bf16[1,197,256]{2,1,0:T(8,128)(2,1)} %param.12) | copy-start | bytes 302596
  61.8 21.3 %copy-start.16 = (f32[1024]{0:T(1024)S(1)}, f32[1024]{0:T(1024)}, u32[]{:S(2)}) copy-start(f32[1024]{0:T(1024)} %param.15) | copy-start | bytes 12292
  63.1 20.0 %copy-start.12 = (bf16[1,197,256]{2,1,0:T(8,128)(2,1)}, bf16[1,197,256]{2,1,0:T(8,128)(2,1)S(1)}, u32[]{:S(2)}) copy-start(bf16[1,197,256]{2,1,0:T(8,128)(2,1)S(1)} %fusion.47) | copy-start | bytes 302596
  72.2 10.9 %copy-start.6 = (bf16[1024,3,256]{2,0,1:T(8,128)(2,1)S(1)}, bf16[1024,3,256]{2,0,1:T(8,128)(2,1)}, u32[]{:S(2)}) copy-start(bf16[1024,3,256]{2,0,1:T(8,128)(2,1)} %param.17) | copy-start | bytes 4718596
  72.3 0.6 copy-start.10
  90.9 1.6 copy-start.7
  92.4 2.7 %copy-start.17 = (f32[1024]{0:T(1024)S(1)}, f32[1024]{0:T(1024)}, u32[]{:S(2)}) copy-start(f32[1024]{0:T(1024)} %param.15) | copy-start | bytes 12292
  99.4 2.5 %copy-start.2 = (bf16[1024,197]{1,0:T(8,128)(2,1)S(1)}, bf16[1024,197]{1,0:T(8,128)(2,1)}, u32[]{:S(2)}) copy-start(bf16[1024,197]{1,0:T(8,128)(2,1)} %copy.117) | copy-start | bytes 1210372
  99.4 3.2 %copy-start.1 = (bf16[8,2,4,16,1024]{4,3,2,1,0:T(8,128)(2,1)S(1)}, bf16[8,2,4,16,1024]{4,3,2,1,0:T(8,128)(2,1)}, u32[]{:S(2)}) copy-start(bf16[8,2,4,16,1024]{4,3,2,1,0:T(8,128)(2,1)} %convolution_convert_fusion.1) | copy-start | bytes 6291460
  113.6 71.1 %copy-start.8 = (bf16[4,64,197]{2,1,0:T(8,128)(2,1)S(1)}, bf16[4,64,197]{2,1,0:T(8,128)(2,1)}, u32[]{:S(2)}) copy-start(bf16[4,64,197]{2,1,0:T(8,128)(2,1)} %convolution_convert_fusion.9) | copy-start | bytes 302596
  115.7 76.1 %all-to-all-start.4 = ((bf16[4,197,256]{2,1,0:T(8,128)(2,1)}), bf16[4,197,256]{2,1,0:T(8,128)(2,1)S(1)}, u32[]{:S(2)}, u32[]{:S(2)}) async-start(bf16[4,197,256]{2,1,0:T(8,128)(2,1)} %bitcast.208), calls=%async_computation.4 | async-start | bytes 819200 | tf_op jit(solution)/shard_map/all_to_all | solution.py:23
  119.1 105.1 %reduce-scatter.6.cloned.1.call-start = ((), (), s32[]{:S(2)}) async-start(), calls=%async_computation.11 | async-start | bytes 983040 | tf_op jit(solution)/shard_map/reduce_scatter | solution.py:64
  188.8 20.3 %copy-start.18 = (f32[256]{0:T(256)S(1)}, f32[256]{0:T(256)}, u32[]{:S(2)}) copy-start(f32[256]{0:T(256)} %get-tuple-element.57) | copy-start | bytes 3076
  188.8 20.3 %copy-start.19 = (f32[1024]{0:T(1024)S(1)}, f32[1024]{0:T(1024)}, u32[]{:S(2)}) copy-start(f32[1024]{0:T(1024)} %get-tuple-element.75) | copy-start | bytes 12292
  191.8 31.7 %copy-start.9 = (bf16[1,197,256]{2,1,0:T(8,128)(2,1)S(1)}, bf16[1,197,256]{2,1,0:T(8,128)(2,1)}, u32[]{:S(2)}) copy-start(bf16[1,197,256]{2,1,0:T(8,128)(2,1)} %param.11) | copy-start | bytes 302596
  191.8 32.5 %copy-start.11 = (bf16[1,197,256]{2,1,0:T(8,128)(2,1)S(1)}, bf16[1,197,256]{2,1,0:T(8,128)(2,1)}, u32[]{:S(2)}) copy-start(bf16[1,197,256]{2,1,0:T(8,128)(2,1)} %param.14) | copy-start | bytes 302596
  191.8 13.5 %all-to-all-start.3 = ((bf16[4,197,256]{2,1,0:T(8,128)(2,1)}), bf16[4,197,256]{2,1,0:T(8,128)(2,1)S(1)}, u32[]{:S(2)}, u32[]{:S(2)}) async-start(bf16[4,197,256]{2,1,0:T(8,128)(2,1)} %bitcast.209), calls=%async_computation.3 | async-start | bytes 819200 | tf_op jit(solution)/shard_map/all_to_all | solution.py:23
  205.9 8.5 %all-to-all-start.5 = ((f32[4,1,394]{2,1,0:T(1,128)}), f32[4,1,394]{2,1,0:T(1,128)S(1)}, u32[]{:S(2)}, u32[]{:S(2)}) async-start(f32[4,1,394]{2,1,0:T(1,128)} %broadcast_in_dim.7), calls=%async_computation.5 | async-start | bytes 16384 | tf_op jit(solution)/shard_map/all_to_all | solution.py:29
  215.4 22.5 %all-to-all-start.6 = ((f32[64,1,1536]{2,1,0:T(1,128)}), f32[64,1,1536]{2,1,0:T(1,128)S(1)}, u32[]{:S(2)}, u32[]{:S(2)}) async-start(f32[64,1,1536]{2,1,0:T(1,128)} %broadcast_in_dim.8), calls=%async_computation.9 | async-start | bytes 786432 | tf_op jit(solution)/shard_map/all_to_all | solution.py:29
  223.3 19.0 %reduce-scatter.8.cloned.1.call-start = ((), (), s32[]{:S(2)}) async-start(), calls=%async_computation.12 | async-start | bytes 294912 | tf_op jit(solution)/shard_map/reduce_scatter | solution.py:64
Sparse Core Ops, SparseCore 0:
  108.4 76.2 reduce-scatter.3
  187.2 21.4 reduce-scatter.5
  226.6 15.6 reduce-scatter.7
where the time goes:
time: 254 us; the launch traced here: 252 us
  waiting for transfers between devices  107 us (42%)
  starting transfers between devices  31.3 us (12%)
  local copies, waits for them, and re-layouts  31.1 us (12%)
  matrix products  29.1 us (11%)
  blocking collectives  20.4 us (8%)
  other arithmetic  18.4 us (7%)
  between operations  14.2 us (6%)
    reduce_scatter x3, waiting for transfers between devices, sum_in_order(): pieces = lax.psum_scatter(pieces, axes[k], scatter_dimension=0, tiled=True)  68.5 us
    all_gather x2, blocking collectives, side_by_side(): whole = lax.all_gather(both, axis, axis=dim, tiled=True)  20.4 us
    all_to_all x3, waiting for transfers between devices, sent_to_all(): return lax.all_to_all(copies, axis, split_axis=0, concat_axis=0, tiled=True)  17.1 us
    all_to_all x3, starting transfers between devices, sent_to_all(): return lax.all_to_all(copies, axis, split_axis=0, concat_axis=0, tiled=True)  14.5 us
    all_to_all x3, waiting for transfers between devices, summed_on_arrival(): lax.all_to_all(pieces, axis, split_axis=0, concat_axis=0, tiled=True)  12.4 us
    all_to_all x3, starting transfers between devices, summed_on_arrival(): lax.all_to_all(pieces, axis, split_axis=0, concat_axis=0, tiled=True)  12 us
    reshape x8, local copies, waits for them, and re-layouts, split_up(): x.reshape(*dims[:dim], devices, dims[dim] // devices, *dims[dim + 1:])  11.2 us
    all_to_all x1, waiting for transfers between devices, summed_on_arrival_2(): pieces = lax.all_to_all(split_up(x, dim, devices), axis, 0, 0, tiled=True)  9.06 us
  transfers between devices with their start and end apart: 10, of which 7 were waited for; matrix products, arithmetic and copies ran while one was open for 15% of the time, Pallas kernels for 0%

commit v1 on v0

v1 whole, which is shorter than its diff:
```python
import functools

import jax
import jax.numpy as jnp
from jax import lax
from jax.experimental import pallas as pl
from jax.experimental.pallas import tpu as pltpu
from jax.sharding import Mesh
from jax.sharding import PartitionSpec as P

AXES = ("z", "yl", "x", "yh", "c")
DP = ("z", "yl", "x")
TENSOR = ("yh", "c")
MESH = pl.DeviceIdType.MESH
SEQ = 197
R = 208
K = 256
W = 256
NZ, NX = 8, 4
EPS = 1e-06
F32 = jnp.float32
BF16 = jnp.bfloat16
GELU_A = 0.7978845608028654
GELU_B = 0.044715
SEMS = 160


def nn(a, b):
    return lax.dot_general(a, b, (((1,), (0,)), ((), ())), preferred_element_type=F32)


def nt(a, b):
    return lax.dot_general(a, b, (((1,), (1,)), ((), ())), preferred_element_type=F32)


def at_cols(ref, lo, hi):
    return ref.at[(slice(None),) * (len(ref.shape) - 1) + (slice(lo, hi),)]


def add_into(dst, src):
    lead = dst.shape[:-2]
    total = 1
    for n in lead:
        total *= n
    if total == 1:
        where = (0,) * len(lead)
        dst[where] = dst[where] + src[where]
        return

    def body(j, _):
        where = []
        rest = j
        for n in reversed(lead):
            where.append(lax.rem(rest, n))
            rest = lax.div(rest, n)
        where = tuple(reversed(where))
        dst[where] = dst[where] + src[where]
        return 0

    lax.fori_loop(0, total, body, 0)


class Chain:
    def __init__(self, net, chunk, axis, size, recv):
        self.net, self.chunk, self.axis, self.size, self.recv = net, chunk, axis, size, recv
        self.pos = net.pos[axis]
        self.steps = size // 2
        self.flying = None

    def part(self, ref, way, distance):
        if distance == self.steps:
            half = ref.shape[-1] // 2
            return at_cols(ref, way * half, (way + 1) * half)
        return ref

    def owner(self, way, distance):
        return lax.rem(self.pos + (distance if way == 0 else self.size - distance), self.size)

    def send(self, way, step):
        distance = self.steps - step + 1
        src = self.part(self.chunk(self.owner(way, distance)), way, distance)
        dst = self.part(self.recv.at[way, step - 1], way, distance)
        target = self.net.dev(**{self.axis: self.owner(way, 1)})
        return self.net.copy(src, dst, target)

    def start(self):
        self.flying = [self.send(0, 1), self.send(1, 1)]

    def tick(self, step):
        later = [None, None]
        for way in (0, 1):
            distance = self.steps - step + 1
            self.flying[way].wait_recv()
            got = self.part(self.recv.at[way, step - 1], way, distance)
            mine = self.part(self.chunk(self.owner(way, distance - 1)), way, distance)
            add_into(mine, got)
            if step < self.steps:
                later[way] = self.send(way, step + 1)
        self.flying = later


class Scatter:
    def __init__(self, net, buf, first, r1, r2, r3, finish):
        z, x, yl = net.pos["z"], net.pos["x"], net.pos["yl"]
        self.net, self.r3, self.finish = net, r3, finish
        if first == "z":
            one = Chain(net, lambda o: buf.at[o], "z", NZ, r1)
            two = Chain(net, lambda o: buf.at[z, :, o], "x", NX, r2)
            self.last = lambda y: buf.at[z, y, x]
        else:
            one = Chain(net, lambda o: buf.at[o], "x", NX, r1)
            two = Chain(net, lambda o: buf.at[x, o], "z", NZ, r2)
            self.last = lambda y: buf.at[x, z, y]
        self.one, self.two, self.yl = one, two, yl
        self.todo = [one.start]
        for s in range(1, one.steps + 1):
            self.todo.append(functools.partial(one.tick, s))
        self.todo.append(two.start)
        for s in range(1, two.steps + 1):
            self.todo.append(functools.partial(two.tick, s))
        self.todo.append(self.start_last)
        self.todo.append(self.end_last)
        merged, k = [[self.todo[0]]], 1
        for f in self.todo[1:]:
            if f == two.start or f == self.start_last:
                merged[-1].append(f)
            else:
                merged.append([f])
        self.todo = merged

    def start_last(self):
        self.flying = self.net.copy(
            self.last(1 - self.yl), self.r3, self.net.dev(yl=1 - self.yl)
        )

    def end_last(self):
        self.flying.wait_recv()
        self.finish(self.last(self.yl)[...].astype(F32) + self.r3[...].astype(F32))

    def tick(self):
        if self.todo:
            for f in self.todo.pop(0):
                f()


class Everyone:
    def __init__(self, net, slots, finish):
        self.net, self.slots, self.finish = net, slots, finish
        self.stages = [("z", NZ), ("x", NX), ("yl", 2)]
        self.at = 0

    def send(self, block):
        axis, n = self.stages[self.at]
        me = self.net.pos[axis]
        slot = self.slots[self.at]
        slot[me] = block
        self.flying = []
        for k in range(1, n):
            target = self.net.dev(**{axis: lax.rem(me + k, n)})
            self.flying.append(self.net.copy(slot.at[me], slot.at[me], target))

    def tick(self):
        if self.at == 3:
            return
        for c in self.flying:
            c.wait_recv()
        slot = self.slots[self.at]
        total = slot[0]
        for k in range(1, self.stages[self.at][1]):
            total = total + slot[k]
        self.at += 1
        if self.at == 3:
            self.finish(total)
        else:
            self.send(total)


class Net:
    def __init__(self, send_sem, recv_sem):
        self.pos = {a: lax.axis_index(a) for a in AXES}
        self.send_sem, self.recv_sem = send_sem, recv_sem
        self.started = []

    def dev(self, **other):
        where = dict(self.pos)
        where.update(other)
        return tuple(where[a] for a in AXES)

    def copy(self, src, dst, target):
        k = len(self.started)
        assert k < SEMS
        c = pltpu.make_async_remote_copy(
            src_ref=src,
            dst_ref=dst,
            send_sem=self.send_sem.at[k],
            recv_sem=self.recv_sem.at[k],
            device_id=target,
            device_id_type=MESH,
        )
        c.start()
        self.started.append(c)
        return c

    def drain(self):
        for c in self.started:
            c.wait_send()


def kernel(
    of_ref, os_ref, gf_ref, gs_ref, gain_attn_ref, gain_mlp_ref, wq_hbm, wp_hbm, wi_hbm, bias_ref, wo_hbm,
    o_first, o_second, o_bfirst, o_bsecond, o_qkv, o_proj, o_inner, o_bias, o_outer, o_gattn, o_gmlp,
    wq, wp, wi, wo, w_sem, send_sem, recv_sem,
    xg, gg, xs, xb, nm, im, act, dg, gh, lhs_a, lhs_b,
    pair_a, pair_b, pair_c, pair_d, mine_a, mine_b, out_a, out_b, out_c, out_d, in_a, in_b, in_c, in_d,
    stat_a, stat_b, qs, ks, vs, hs, rows_s, g3,
    ga, gb, ra1, ra2, ra3, rb1, rb2, rb3,
    ha, hb, sa1, sa2, sa3, sb1, sb2, sb3,
    t1z, t1x, t1y, t2z, t2x, t2y,
):
    net = Net(send_sem, recv_sem)
    pos = net.pos
    yh, c = pos["yh"], pos["c"]
    me, sib = 2 * yh + c, 2 * yh + 1 - c
    far, diag = 2 * (1 - yh) + c, 2 * (1 - yh) + 1 - c
    d_sib, d_far, d_diag = net.dev(c=1 - c), net.dev(yh=1 - yh), net.dev(yh=1 - yh, c=1 - c)

    barrier = pltpu.get_barrier_semaphore()
    others = [d_sib, d_far, d_diag, net.dev(yl=1 - pos["yl"])]
    others += [net.dev(z=lax.rem(pos["z"] + k, NZ)) for k in range(1, NZ)]
    others += [net.dev(x=lax.rem(pos["x"] + k, NX)) for k in range(1, NX)]
    for other in others:
        pl.semaphore_signal(barrier, inc=1, device_id=other, device_id_type=MESH)

    loads = [
        pltpu.make_async_copy(wi_hbm, wi, w_sem.at[0]),
        pltpu.make_async_copy(wo_hbm, wo, w_sem.at[1]),
        pltpu.make_async_copy(wq_hbm, wq, w_sem.at[2]),
        pltpu.make_async_copy(wp_hbm, wp, w_sem.at[3]),
    ]
    for load in loads:
        load.start()

    zero_rows = jnp.zeros((K - R, W), BF16)
    xg[me] = jnp.zeros((R, W), BF16)
    xg[me, 0:SEQ] = of_ref[...]
    gg[me, 0:R] = jnp.zeros((R, W), BF16)
    gg[me, 0:SEQ] = gs_ref[...]
    pl.semaphore_wait(barrier, len(others))

    def gather_start(ref, block=None):
        own = ref.at[me, 0:R]
        return [net.copy(own, own, d_far), net.copy(own, own, d_sib)]

    def gather_forward(ref, two):
        two[0].wait_recv()
        got = ref.at[far, 0:R]
        two.append(net.copy(got, got, d_sib))

    def gather_end(two):
        two[1].wait_recv()
        two[2].wait_recv()

    x_all = gather_start(xg)
    g_all = gather_start(gg)
    for b in range(4):
        gg[b, R:K] = zero_rows
        xb[b, R:K] = zero_rows
        for ref in (im, act, gh):
            ref[R:K, b * W : (b + 1) * W] = zero_rows
    for ref in (qs, ks, vs, hs):
        ref[R:K] = zero_rows
    gather_forward(xg, x_all)
    gather_end(x_all)

    def gain_of(ref, b):
        return ref[0:1, b * W : (b + 1) * W]

    def gain_at(ref, b):
        return ref[0:1, pl.ds(pl.multiple_of(b * W, W), W)]

    def normalize(block, gain_ref):
        total = jnp.zeros((R, 1), F32)
        for b in range(4):
            total = total + jnp.sum(block(b), 1, keepdims=True)
        mean = total * (1.0 / 1024)
        square = jnp.zeros((R, 1), F32)
        for b in range(4):
            centre = block(b) - mean
            nm[b] = centre
            square = square + jnp.sum(centre * centre, 1, keepdims=True)
        spread = lax.rsqrt(square * (1.0 / 1024) + EPS)
        for b in range(4):
            normed = nm[b] * spread
            nm[b] = normed
            im[0:R, b * W : (b + 1) * W] = (normed * gain_of(gain_ref, b)).astype(BF16)
        return spread

    spread_mlp = normalize(lambda b: xg[b].astype(F32), gain_mlp_ref)

    loads[0].wait()
    for n in range(4):
        cols = slice(n * W, (n + 1) * W)
        u = nn(im[0:R], wi[:, cols]) + bias_ref[0:1, cols]
        square = u * u
        t = jnp.tanh(GELU_A * (u + GELU_B * (square * u)))
        half = 0.5 * (1.0 + t)
        act[0:R, cols] = (u * half).astype(BF16)
        slope = 0.5 * GELU_A * (1.0 - t * t) * (1.0 + 3.0 * GELU_B * square)
        dg[0:R, cols] = half + u * slope
        if n == 1:
            gather_forward(gg, g_all)

    loads[1].wait()

    def rows_at(ref, q):
        return ref[pl.ds(pl.multiple_of(q * W, W), W), :]

    pair_a[0, 0] = nt(act[0:R], rows_at(wo, sib))
    pair_a[0, 1] = nt(act[0:R], rows_at(wo, diag))
    pair_mlp = net.copy(pair_a.at[0], pair_a.at[1], d_sib)
    mine_a[0] = nt(act[0:R], rows_at(wo, far))
    mine_a[1] = nt(act[0:R], rows_at(wo, me))
    pair_mlp.wait_recv()
    out_a[...] = (mine_a[0] + pair_a[1, 1]).astype(BF16)
    far_mlp = net.copy(out_a, in_a, d_far)
    gather_end(g_all)

    for n in range(4):
        cols = slice(n * W, (n + 1) * W)
        grad_active = nn(gg[0, 0:R], wo[0:W, cols])
        for b in range(1, 4):
            grad_active = grad_active + nn(gg[b, 0:R], wo[b * W : (b + 1) * W, cols])
        low = (grad_active * dg[0:R, cols]).astype(BF16)
        gh[0:R, cols] = low
        o_bias[0:1, cols] = jnp.sum(low.astype(F32), 0, keepdims=True)

    lane = lax.broadcasted_iota(jnp.int32, (R, 128), 1)

    def stats_of(part, q, gain_ref, sums):
        scaled = part * gain_at(gain_ref, q)
        one = sums[0] + jnp.sum(scaled, 1, keepdims=True)
        two = sums[1] + jnp.sum(scaled * nm[q], 1, keepdims=True)
        return (one, two)

    def stats_send(sums, stat):
        both = jnp.where(lane == 0, sums[0], jnp.where(lane == 1, sums[1], 0.0))
        both = jnp.concatenate([both, jnp.zeros((K - R, 128), F32)], 0)
        stat[me] = both.T[0:8, :]
        return [net.copy(stat.at[me], stat.at[me], d) for d in (d_sib, d_far, d_diag)]

    def stats_end(sent, stat):
        for s in sent:
            s.wait_recv()
        total = (stat[0] + stat[1]) + (stat[2] + stat[3])
        wide = jnp.concatenate([total * (1.0 / 1024), jnp.zeros((120, K), F32)], 0).T
        return wide[0:R, 0:1], wide[0:R, 1:2]

    def norm_back(part_of, gain_ref, pair, mine, out, inn, stat, between):
        sums = (jnp.zeros((R, 1), F32), jnp.zeros((R, 1), F32))
        for slot, q in ((0, sib), (1, diag)):
            part = part_of(q)
            pair[0, slot] = part
            sums = stats_of(part, q, gain_ref, sums)
        swap = net.copy(pair.at[0], pair.at[1], d_sib)
        for slot, q in ((0, far), (1, me)):
            part = part_of(q)
            mine[slot] = part
            sums = stats_of(part, q, gain_ref, sums)
        sent = stats_send(sums, stat)
        swap.wait_recv()
        out[...] = (mine[0] + pair[1, 1]).astype(BF16)
        last = net.copy(out, inn, d_far)
        between()
        last.wait_recv()
        first_mean, second_mean = stats_end(sent, stat)
        grad = mine[1] + pair[1, 0] + inn[...].astype(F32)
        return grad, first_mean, second_mean

    ends = {}
    valid = lax.broadcasted_iota(jnp.int32, (R, W), 0) < SEQ

    def outer_term(lhs, rhs, buf, first, col):
        for b in range(4):
            tile = nn(lhs[b * W : (b + 1) * W], rhs).astype(BF16).reshape(2, 2, 4, 16, W)
            if first == "z":
                buf[2 * b : 2 * b + 2, :, :, :, col : col + W] = tile
            else:
                for x in range(4):
                    buf[x, 2 * b : 2 * b + 2, :, :, col : col + W] = tile[:, :, x]

    def finish_outer(total):
        o_outer[...] = total

    def finish_inner(total):
        o_inner[...] = total

    def finish_ha(total):
        o_proj[...] = total[:, 0:W]
        o_qkv[2] = total[:, W : 2 * W]

    def finish_hb(total):
        o_qkv[0] = total[:, 0:W]
        o_qkv[1] = total[:, W : 2 * W]

    def finish_small1(total):
        for n in range(4):
            o_bias[0:1, n * W : (n + 1) * W] = total[n : n + 1]
        o_gmlp[...] = total[4:5]

    def finish_small2(total):
        o_gattn[...] = total[0:1]

    s_outer = Scatter(net, ga, "z", ra1, ra2, ra3, finish_outer)
    s_inner = Scatter(net, gb, "x", rb1, rb2, rb3, finish_inner)
    s_ha = Scatter(net, ha, "z", sa1, sa2, sa3, finish_ha)
    s_hb = Scatter(net, hb, "x", sb1, sb2, sb3, finish_hb)
    small1 = Everyone(net, (t1z, t1x, t1y), finish_small1)
    small2 = Everyone(net, (t2z, t2x, t2y), finish_small2)

    def between_mlp():
        far_mlp.wait_recv()
        mlp = mine_a[1] + pair_a[1, 0] + in_a[...].astype(F32)
        os_wide = os_ref[...].astype(F32)
        second = jnp.where(valid[0:SEQ], os_wide - mlp[0:SEQ], 0.0).astype(BF16)
        o_second[...] = second
        xs[me] = jnp.zeros((R, W), BF16)
        xs[me, 0:SEQ] = second
        ends["second"] = gather_start(xs)
        for b in range(4):
            lhs_a[b * W : (b + 1) * W] = gg[b].T
        for n in range(4):
            outer_term(lhs_a, act[:, n * W : (n + 1) * W], ga, "z", n * W)
        s_outer.tick()

    grad, first_mean, second_mean = norm_back(
        lambda q: nt(gh[0:R], rows_at(wi, q)),
        gain_mlp_ref, pair_b, mine_b, out_b, in_b, stat_a, between_mlp,
    )
    normed_own = nm[me]
    back = spread_mlp * (grad * gain_at(gain_mlp_ref, me) - first_mean - normed_own * second_mean)
    first = (gf_ref[...].astype(F32) + back[0:SEQ]).astype(BF16)
    o_bfirst[...] = first
    xb[me, 0:R] = jnp.zeros((R, W), BF16)
    xb[me, 0:SEQ] = first
    b_all = gather_start(xb)
    gather_forward(xs, ends["second"])
    block = [o_bias[0:1, n * W : (n + 1) * W] for n in range(4)]
    block.append(jnp.sum(grad * normed_own, 0, keepdims=True))
    small1.send(jnp.concatenate(block + [jnp.zeros((3, W), F32)], 0))

    for b in range(4):
        lhs_b[b * W : (b + 1) * W] = im[:, b * W : (b + 1) * W].T
    for n in range(4):
        outer_term(lhs_b, gh[:, n * W : (n + 1) * W], gb, "x", n * W)
    s_inner.tick()
    gather_end(ends["second"])

    spread_attn = normalize(lambda b: xs[b].astype(F32), gain_attn_ref)
    gather_forward(xb, b_all)
    s_outer.tick()
    loads[2].wait()
    for kind, ref in enumerate((qs, ks, vs)):
        ref[0:R] = nn(im[0:R], wq[kind]).astype(BF16)
    for b in range(4):
        lhs_a[b * W : (b + 1) * W] = im[:, b * W : (b + 1) * W].T
    small1.tick()
    gather_end(b_all)
    loads[3].wait()
    heads = nn(xb[0, 0:R], wp[0:W])
    for b in range(1, 4):
        heads = heads + nn(xb[b, 0:R], wp[b * W : (b + 1) * W])
    hs[0:R] = heads.astype(BF16)
    for b in range(4):
        lhs_b[b * W : (b + 1) * W] = xb[b].T
    s_inner.tick()
    s_outer.tick()

    head_lane = lax.broadcasted_iota(jnp.int32, (K, W), 1) // 64
    key_ok = lax.broadcasted_iota(jnp.int32, (K, K), 1) < SEQ
    factor = 0.125

    def only(ref, h):
        return jnp.where(head_lane == h, ref[...], jnp.zeros((), BF16))

    attn = jnp.zeros((K, W), F32)
    grads = [jnp.zeros((K, W), F32) for _ in range(3)]
    for h in range(4):
        q_h, k_h, v_h, g_h = only(qs, h), only(ks, h), only(vs, h), only(hs, h)
        scores = jnp.where(key_ok, nt(q_h, ks[...]) * factor, -1e30)
        e = jnp.exp(scores - jnp.max(scores, 1, keepdims=True))
        probs = e / jnp.sum(e, 1, keepdims=True)
        low = probs.astype(BF16)
        grad_probs = nt(g_h, vs[...])
        row_dot = jnp.sum(grad_probs * probs, 1, keepdims=True)
        grad_scores = (probs * (grad_probs - row_dot)).astype(BF16)
        a_h = nn(low, v_h)
        gv_h = nn(low.T, g_h)
        gq_h = nn(grad_scores, k_h)
        gk_h = nn(grad_scores.T, q_h)
        if h == 0:
            rows_s[0], rows_s[1], rows_s[2], rows_s[3] = a_h, gq_h, gk_h, gv_h
        else:
            rows_s[0] += a_h
            rows_s[1] += gq_h
            rows_s[2] += gk_h
            rows_s[3] += gv_h
        if h == 1:
            small1.tick()
    rows_low = rows_s[0].astype(BF16)
    g3[0] = (rows_s[1] * factor).astype(BF16)
    g3[1] = (rows_s[2] * factor).astype(BF16)
    g3[2] = rows_s[3].astype(BF16)

    for slot, q in ((0, sib), (1, diag)):
        pair_c[0, slot] = nt(rows_low[0:R], rows_at(wp, q))
    pair_out = net.copy(pair_c.at[0], pair_c.at[1], d_sib)
    for slot, q in ((0, far), (1, me)):
        mine_a[slot] = nt(rows_low[0:R], rows_at(wp, q))
    s_outer.tick()
    pair_out.wait_recv()
    out_c[...] = (mine_a[0] + pair_c[1, 1]).astype(BF16)
    far_out = net.copy(out_c, in_c, d_far)

    outer_term(lhs_b, rows_low, ha, "z", 0)
    outer_term(lhs_a, g3[2], ha, "z", W)
    s_ha.tick()
    outer_term(lhs_a, g3[0], hb, "x", 0)
    outer_term(lhs_a, g3[1], hb, "x", W)
    s_hb.tick()
    small1.tick()

    def qkv_part(q):
        at = pl.ds(pl.multiple_of(q * W, W), W)
        part = nt(g3[0, 0:R], wq[0, at, :])
        part = part + nt(g3[1, 0:R], wq[1, at, :])
        return part + nt(g3[2, 0:R], wq[2, at, :])

    def between_attn():
        far_out.wait_recv()
        total = mine_a[1] + pair_c[1, 0] + in_c[...].astype(F32)
        o_first[...] = (of_ref[...].astype(F32) - total[0:SEQ]).astype(BF16)
        s_outer.tick()
        s_inner.tick()

    grad, first_mean, second_mean = norm_back(
        qkv_part, gain_attn_ref, pair_d, mine_b, out_d, in_d, stat_b, between_attn
    )
    normed_own = nm[me]
    small2.send(
        jnp.concatenate([jnp.sum(grad * normed_own, 0, keepdims=True), jnp.zeros((7, W), F32)], 0)
    )
    back = spread_attn * (grad * gain_at(gain_attn_ref, me) - first_mean - normed_own * second_mean)
    o_bsecond[...] = (gs_ref[...].astype(F32) + back[0:SEQ]).astype(BF16)

    for _ in range(8):
        s_ha.tick()
        s_hb.tick()
        small2.tick()
        s_outer.tick()
        s_inner.tick()
    assert not (s_ha.todo or s_hb.todo or s_outer.todo or s_inner.todo)
    assert small1.at == 3 and small2.at == 3
    net.drain()


def on_device(
    out_first, out_second, grad_first, grad_second, gain_attn, gain_mlp,
    qkv_weight, proj_weight, inner_weight, inner_bias, outer_weight,
):
    sds = jax.ShapeDtypeStruct
    vmem = pl.BlockSpec(memory_space=pltpu.VMEM)
    hbm = pl.BlockSpec(memory_space=pl.ANY)

    def v(*shape, dtype=BF16):
        return pltpu.VMEM(shape, dtype)

    def scatter_bufs(cols):
        a = [v(8, 2, 4, 16, cols), v(4, 8, 2, 16, cols)]
        za = [v(2, 4, 2, 4, 16, cols), v(2, 2, 2, 16, cols), v(16, cols)]
        xb = [v(2, 2, 8, 2, 16, cols), v(2, 4, 2, 16, cols), v(16, cols)]
        return a + za + xb

    scratch = [
        v(3, 1024, W), v(1024, W), v(1024, 1024), v(1024, 1024), pltpu.SemaphoreType.DMA((4,)),
        pltpu.SemaphoreType.DMA((SEMS,)), pltpu.SemaphoreType.DMA((SEMS,)),
        v(4, R, W), v(4, K, W), v(4, R, W), v(4, K, W), v(4, R, W, dtype=F32),
        v(K, 1024), v(K, 1024), v(R, 1024, dtype=F32), v(K, 1024), v(1024, K), v(1024, K),
        *[v(2, 2, R, W, dtype=F32) for _ in range(4)],
        *[v(2, R, W, dtype=F32) for _ in range(2)],
        *[v(R, W) for _ in range(8)],
        v(4, 8, K, dtype=F32), v(4, 8, K, dtype=F32),
        *[v(K, W) for _ in range(4)],
        v(4, K, W, dtype=F32), v(3, K, W),
        *scatter_bufs(1024), *scatter_bufs(512),
        *[v(n, 8, W, dtype=F32) for n in (8, 4, 2, 8, 4, 2)],
    ]
    outs = pl.pallas_call(
        kernel,
        out_shape=[
            sds((SEQ, W), BF16), sds((SEQ, W), BF16), sds((SEQ, W), BF16), sds((SEQ, W), BF16),
            sds((3, 16, W), F32), sds((16, W), F32), sds((16, 1024), F32), sds((1, 1024), F32),
            sds((16, 1024), F32), sds((1, W), F32), sds((1, W), F32),
        ],
        in_specs=[vmem] * 6 + [hbm] * 3 + [vmem, hbm],
        out_specs=[vmem] * 11,
        scratch_shapes=scratch,
        compiler_params=pltpu.CompilerParams(
            collective_id=0, has_side_effects=True, vmem_limit_bytes=60 * 1024 * 1024
        ),
        name="block_pair",
    )(
        out_first[0], out_second[0], grad_first[0], grad_second[0],
        gain_attn.reshape(1, -1), gain_mlp.reshape(1, -1),
        jnp.swapaxes(qkv_weight, 0, 1), proj_weight, inner_weight, inner_bias.reshape(1, -1), outer_weight,
    )
    return (
        outs[0][None], outs[1][None], outs[2][None], outs[3][None],
        jnp.swapaxes(outs[4], 0, 1), outs[5], outs[6], outs[7].reshape(-1), outs[8],
        outs[9].reshape(-1), outs[10].reshape(-1),
    )


def solution(mesh):
    split = Mesh(mesh.devices.reshape(NZ, 2, NX, 2, 2), AXES)
    rows = P(DP, None, TENSOR)
    return jax.shard_map(
        on_device,
        mesh=split,
        in_specs=(
            rows, rows, rows, rows, P(), P(),
            P(None, None, TENSOR), P(None, TENSOR), P(None, TENSOR), P(TENSOR), P(None, TENSOR),
        ),
        out_specs=(
            rows, rows, rows, rows,
            P(DP, None, TENSOR), P(DP, TENSOR), P(DP, TENSOR), P(TENSOR), P(DP, TENSOR),
            P(TENSOR), P(TENSOR),
        ),
        check_vma=False,
    )
```

time: 254 us -> 104 us (0.41)
  waiting for transfers between devices: 107 us -> 0 us
  Pallas kernels: 0 us -> 86.1 us
  starting transfers between devices: 31.3 us -> 0 us
  matrix products: 29.1 us -> 0 us
  blocking collectives: 20.4 us -> 0 us
  other arithmetic: 18.4 us -> 0 us
  local copies, waits for them, and re-layouts: 31.1 us -> 15.5 us
  between operations: 14.2 us -> 0.66 us
    pallas_call x0 -> x1, Pallas kernels: none -> 86.1 us  [on_device(): pl.pallas_call(kernel, out_shape=[sds((SEQ, W), BF16), sds((SEQ, W), BF16...]
    reduce_scatter x3 -> x0, waiting for transfers between devices: 68.5 us -> none  [sum_in_order(): pieces = lax.psum_scatter(pieces, axes[k], scatter_dimension=0, tiled=True)]
    all_to_all x7 -> x0, waiting for transfers between devices: 38.6 us -> none  [the longest x3 17.1 us: sent_to_all(): return lax.all_to_all(copies, axis, split_axis=0, concat_axis=0, tiled=True)]
    all_to_all x7 -> x0, starting transfers between devices: 31.2 us -> none  [the longest x3 14.5 us: sent_to_all(): return lax.all_to_all(copies, axis, split_axis=0, concat_axis=0, tiled=True)]
    dot_general x17 -> x0, matrix products: 27.7 us -> none  [the longest x4 8.37 us: weight_term(): lax.dot_general(left_rows, right_rows, (((0,), (0,)), ((), ())), preferre...]
    all_gather x2 -> x0, blocking collectives: 20.4 us -> none  [side_by_side(): whole = lax.all_gather(both, axis, axis=dim, tiled=True)]
    reshape x9 -> x0, local copies, waits for them, and re-layouts: 11.8 us -> none  [the longest x8 11.2 us: split_up(): x.reshape(*dims[:dim], devices, dims[dim] // devices, *dims[dim + 1:])]
    unnamed x45 -> x11, local copies, waits for them, and re-layouts: 4.75 us -> 15.5 us
  transfers between devices with their start and end apart: 10 -> 0, of which waited for: 7 -> 0; matrix products, arithmetic and copies ran while one was open for 15% -> 0% of each run, Pallas kernels for 0% -> 0%
where the time goes in v1:
time: 104 us; the launch traced here: 102 us
  Pallas kernels  86.1 us (83%)
  local copies, waits for them, and re-layouts  15.5 us (15%)
    pallas_call x1, Pallas kernels, on_device(): pl.pallas_call(kernel, out_shape=[sds((SEQ, W), BF16), sds((SEQ, W), BF16...  86.1 us
    unnamed x11, local copies, waits for them, and re-layouts  15.5 us

profile of v1, /device:TPU:2, one launch (start us, length us, event | category | flops | bytes accessed | tf_op | source)
XLA Modules:
  0.0 102.3 jit_solution(5729425382345576899)
XLA Ops:
  0.6 86.1 %block_pair.1 = (bf16[197,256]{1,0:T(8,128)(2,1)}, bf16[197,256]{1,0:T(8,128)(2,1)}, bf16[197,256]{1,0:T(8,128)(2,1)}, bf16[197,256]{1,0:T(8,128)(2,1)}, f32[3,1...) custom-call(bf16[197,256]{1,0:T(8,128)(2,1)} %bitcast.21, ...), custom_call_target="tpu_custom_call" | custom-call | tf_op jit(solution)/shard_map/block_pair/pallas_call | solution.py:597
  86.8 1.5 %copy.33 = bf16[1,197,256]{2,1,0:T(8,128)(2,1)} copy(bf16[1,197,256]{2,1,0:T(8,128)(2,1)} %bitcast.20) | data formatting | bytes 201728
  88.3 1.5 %copy.34 = bf16[1,197,256]{2,1,0:T(8,128)(2,1)} copy(bf16[1,197,256]{2,1,0:T(8,128)(2,1)} %bitcast.19) | data formatting | bytes 201728
  89.8 1.5 %copy.35 = bf16[1,197,256]{2,1,0:T(8,128)(2,1)} copy(bf16[1,197,256]{2,1,0:T(8,128)(2,1)} %bitcast.18) | data formatting | bytes 201728
  91.4 1.5 %copy.36 = bf16[1,197,256]{2,1,0:T(8,128)(2,1)} copy(bf16[1,197,256]{2,1,0:T(8,128)(2,1)} %bitcast.17) | data formatting | bytes 201728
  92.9 1.4 %copy.37 = f32[16,3,256]{2,0,1:T(8,128)} copy(f32[16,3,256]{2,0,1:T(8,128)} %bitcast.25) | data formatting | bytes 98304
  94.4 1.3 %copy.38 = f32[16,256]{1,0:T(8,128)} copy(f32[16,256]{1,0:T(8,128)} %get-tuple-element.49) | data formatting | bytes 32768
  95.7 1.5 %copy.39 = f32[16,1024]{1,0:T(8,128)} copy(f32[16,1024]{1,0:T(8,128)} %get-tuple-element.50) | data formatting | bytes 131072
  97.1 1.3 %copy.40 = f32[1024]{0:T(1024)} copy(f32[1024]{0:T(1024)} %bitcast.26) | data formatting | bytes 8192
  98.4 1.5 %copy.41 = f32[16,1024]{1,0:T(8,128)} copy(f32[16,1024]{1,0:T(8,128)} %get-tuple-element.52) | data formatting | bytes 131072
  99.9 1.2 %copy.42 = f32[256]{0:T(256)} copy(f32[256]{0:T(256)} %bitcast.31) | data formatting | bytes 2048
  101.1 1.2 %copy.43 = f32[256]{0:T(256)} copy(f32[256]{0:T(256)} %bitcast.30) | data formatting | bytes 2048

commit v2 on v1

v2 whole, which is shorter than its diff:
```python
import functools

import jax
import jax.numpy as jnp
from jax import lax
from jax.experimental import pallas as pl
from jax.experimental.pallas import tpu as pltpu
from jax.sharding import Mesh
from jax.sharding import PartitionSpec as P

AXES = ("z", "yl", "x", "yh", "c")
DP = ("z", "yl", "x")
TENSOR = ("yh", "c")
MESH = pl.DeviceIdType.MESH
SEQ = 197
R = 208
K = 256
W = 256
NZ, NX = 8, 4
EPS = 1e-06
F32 = jnp.float32
BF16 = jnp.bfloat16
GELU_A = 0.7978845608028654
GELU_B = 0.044715
SENDS, RECVS = 71, 71
PIECES = (
    ("A1", "outer", "z", 0, 256),
    ("A2", "outer", "z", 256, 512),
    ("B0", "outer", "xz", 512, 1024),
    ("A3", "inner", "z", 0, 256),
    ("B1", "inner", "xz", 256, 1024),
    ("a1", "v", "z", 0, 256),
    ("a2", "proj", "z", 0, 256),
    ("b1", "q", "x", 0, 256),
    ("b2", "k", "x", 0, 256),
)
TICKS = {
    "swap": ("A1", "A2"),
    "inner": ("B0",),
    "back": ("A1", "A2"),
    "forward": ("A3",),
    "qkv": ("B1",),
    "probs": ("A1", "A2"),
    "heads": ("A3", "s1"),
    "attn": ("B0", "A1", "A2"),
    "pair": ("A3", "B0"),
    "last": ("a1", "a2", "s1", "B0", "B1"),
    "tail": (
        "a1", "a2", "b1", "b2", "A3", "A1", "A2", "B0", "B1",
        "a1", "a2", "A3", "B0", "B1", "b1", "b2", "s2",
        "B0", "B1", "a1", "a2", "s2", "B1", "b1", "b2", "B1", "a1", "a2",
    ),
}


def nn(a, b):
    return lax.dot_general(a, b, (((1,), (0,)), ((), ())), preferred_element_type=F32)


def nt(a, b):
    return lax.dot_general(a, b, (((1,), (1,)), ((), ())), preferred_element_type=F32)


def at_cols(ref, lo, hi):
    return ref.at[(slice(None),) * (len(ref.shape) - 1) + (slice(lo, hi),)]


def add_into(dst, src):
    lead = dst.shape[:-2]
    total = 1
    for n in lead:
        total *= n
    if total == 1:
        where = (0,) * len(lead)
        dst[where] = dst[where] + src[where]
        return

    def body(j, _):
        where = []
        rest = j
        for n in reversed(lead):
            where.append(lax.rem(rest, n))
            rest = lax.div(rest, n)
        where = tuple(reversed(where))
        dst[where] = dst[where] + src[where]
        return 0

    lax.fori_loop(0, total, body, 0)


class Phases:
    def __init__(self):
        self.scope = None

    def __call__(self, name):
        if self.scope is not None:
            self.scope.__exit__(None, None, None)
        self.scope = jax.named_scope(name) if name else None
        if name:
            self.scope.__enter__()


class Net:
    def __init__(self, send_sem, recv_sem):
        self.pos = {a: lax.axis_index(a) for a in AXES}
        self.send_sem, self.recv_sem = send_sem, recv_sem
        self.sends, self.recvs = 0, 0
        self.out = []

    def dev(self, **other):
        where = dict(self.pos)
        where.update(other)
        return tuple(where[a] for a in AXES)

    def copies(self, triples, sent, got=None):
        k, m = self.sends, self.recvs
        self.sends, self.recvs = k + 1, m + 1
        assert self.sends <= SENDS and self.recvs <= RECVS

        def describe(src, dst, target):
            return pltpu.make_async_remote_copy(
                src_ref=src,
                dst_ref=dst,
                send_sem=self.send_sem.at[k],
                recv_sem=self.recv_sem.at[m],
                device_id=target,
                device_id_type=MESH,
            )

        for triple in triples:
            describe(*triple).start()
        target = triples[0][2]
        self.out.append(describe(sent, sent, target))
        return describe(sent if got is None else got, sent if got is None else got, target)

    def copy(self, src, dst, target):
        return self.copies([(src, dst, target)], src, dst)

    def drain(self):
        for c in self.out:
            c.wait_send()


class Chain:
    def __init__(self, net, chunk, axis, size, recv):
        self.net, self.chunk, self.axis, self.size, self.recv = net, chunk, axis, size, recv
        self.pos = net.pos[axis]
        self.steps = size // 2

    def part(self, ref, way, distance):
        if distance == self.steps:
            half = ref.shape[-1] // 2
            return at_cols(ref, way * half, (way + 1) * half)
        return ref

    def owner(self, way, distance):
        return lax.rem(self.pos + (distance if way == 0 else self.size - distance), self.size)

    def send(self, step):
        distance = self.steps - step + 1
        triples = []
        for way in (0, 1):
            src = self.part(self.chunk(self.owner(way, distance)), way, distance)
            dst = self.part(self.recv.at[way, step - 1], way, distance)
            triples.append((src, dst, self.net.dev(**{self.axis: self.owner(way, 1)})))
        both = self.recv.at[0, 0] if step == 1 else self.recv.at[:, step - 1]
        self.flying = self.net.copies(triples, both)

    def tick(self, step):
        self.flying.wait_recv()
        distance = self.steps - step + 1
        for way in (0, 1):
            got = self.part(self.recv.at[way, step - 1], way, distance)
            mine = self.part(self.chunk(self.owner(way, distance - 1)), way, distance)
            add_into(mine, got)
        if step < self.steps:
            self.send(step + 1)


class Spread:
    def __init__(self, net, ring, size, recv):
        self.net, self.ring, self.size, self.recv = net, ring, size, recv

    def start(self, piece):
        net, ring, size = self.net, self.ring, self.size
        triples = []
        for j in range(1, 2 * size):
            there = lax.rem(net.pos[ring] + j % size, size)
            y = lax.rem(net.pos["yl"] + j // size, 2)
            triples.append((piece(there, y), self.recv.at[j], net.dev(**{ring: there, "yl": y})))
        self.flying = net.copies(triples, self.recv.at[1 : 2 * size])

    def end(self, own):
        self.flying.wait_recv()
        total = own
        for j in range(1, 2 * self.size):
            total = total + self.recv[j].astype(F32)
        return total


class Scatter:
    def __init__(self, net, first, bufs, finish):
        z, x, yl = net.pos["z"], net.pos["x"], net.pos["yl"]
        buf = bufs[0]
        self.todo = []
        if first == "z":
            one = Chain(net, lambda o: buf.at[o], "z", NZ, bufs[1])
            last = Spread(net, "x", NX, bufs[2])
            piece = lambda there, y: buf.at[z, y, there]
            own = lambda: buf[z, yl, x].astype(F32)
        else:
            one = Chain(net, lambda o: buf.at[o], "x", NX, bufs[1])
            piece = lambda there, y: buf.at[x, there, y]
            own = lambda: buf[x, z, yl].astype(F32)
            if first == "xz":
                two = Chain(net, lambda o: buf.at[x, o], "z", NZ, bufs[2])
            else:
                last = Spread(net, "z", NZ, bufs[2])
        self.todo.append(functools.partial(one.send, 1))
        for k in range(1, one.steps):
            self.todo.append(functools.partial(one.tick, k))
        if first == "xz":

            def turn():
                one.tick(one.steps)
                two.send(1)

            self.todo.append(turn)
            for k in range(1, two.steps):
                self.todo.append(functools.partial(two.tick, k))

            def across():
                two.tick(two.steps)
                self.flying = net.copy(buf.at[x, z, 1 - yl], bufs[3], net.dev(yl=1 - yl))

            def end():
                self.flying.wait_recv()
                finish(own() + bufs[3][...].astype(F32))

            self.todo += [across, end]
        else:

            def turn():
                one.tick(one.steps)
                last.start(piece)

            self.todo += [turn, lambda: finish(last.end(own()))]

    def tick(self):
        self.todo.pop(0)()


class Everyone:
    def __init__(self, net, slots, finish):
        self.net, self.slots, self.finish = net, slots, finish
        self.todo = [self.turn, self.end]

    def send(self, block):
        self.slots[0][0] = block
        self.one = Spread(self.net, "z", NZ, self.slots[0])
        self.one.start(lambda there, y: self.slots[0].at[0])

    def turn(self):
        net, slot = self.net, self.slots[1]
        slot[0] = self.one.end(self.slots[0][0])
        triples = []
        for k in range(1, NX):
            target = net.dev(x=lax.rem(net.pos["x"] + k, NX))
            triples.append((slot.at[0], slot.at[k], target))
        self.flying = net.copies(triples, slot.at[1:NX])

    def end(self):
        self.flying.wait_recv()
        slot = self.slots[1]
        self.finish(((slot[0] + slot[1]) + slot[2]) + slot[3])

    def tick(self):
        self.todo.pop(0)()


def kernel(
    of_hbm, os_hbm, gf_hbm, gs_hbm, gain_attn_hbm, gain_mlp_hbm, wq_hbm, wp_hbm, wi_hbm, bias_hbm, wo_hbm,
    o_first, o_second, o_bfirst, o_bsecond, o_qkv, o_proj, o_inner, o_bias, o_outer, o_gattn, o_gmlp,
    of_ref, os_ref, gf_ref, gs_ref, gain_attn_ref, gain_mlp_ref, wq, wp, wi, bias_ref, wo,
    load_sem, send_sem, recv_sem,
    xg, gg, xs, xb, nm, im, act, dg, gh, lhs_a, lhs_b,
    pair_a, pair_b, pair_c, pair_d, mine_a, mine_b, out_a, out_b, out_c, out_d, in_a, in_b, in_c, in_d,
    stat_a, stat_b, qs, ks, vs, hs, rows_s, probs_s, g3,
    *rest,
):
    phase = Phases()
    phase("entry")
    net = Net(send_sem, recv_sem)
    pos = net.pos
    yh, c = pos["yh"], pos["c"]
    me, sib = 2 * yh + c, 2 * yh + 1 - c
    far, diag = 2 * (1 - yh) + c, 2 * (1 - yh) + 1 - c
    d_sib, d_far, d_diag = net.dev(c=1 - c), net.dev(yh=1 - yh), net.dev(yh=1 - yh, c=1 - c)

    loads = {}
    for k, (name, src, dst) in enumerate(
        (
            ("of", of_hbm, of_ref), ("gs", gs_hbm, gs_ref), ("gm", gain_mlp_hbm, gain_mlp_ref),
            ("bias", bias_hbm, bias_ref), ("wi", wi_hbm, wi), ("wo", wo_hbm, wo), ("os", os_hbm, os_ref),
            ("gf", gf_hbm, gf_ref), ("ga", gain_attn_hbm, gain_attn_ref), ("wq", wq_hbm, wq), ("wp", wp_hbm, wp),
        )
    ):
        loads[name] = pltpu.make_async_copy(src, dst, load_sem.at[k])
        loads[name].start()

    barrier = pltpu.get_barrier_semaphore()
    others = [d_sib, d_far, d_diag]
    for dy in range(2):
        y = lax.rem(pos["yl"] + dy, 2)
        others += [net.dev(z=lax.rem(pos["z"] + k, NZ), yl=y) for k in range(1 - dy, NZ)]
        others += [net.dev(x=lax.rem(pos["x"] + k, NX), yl=y) for k in range(1, NX)]
    for other in others:
        pl.semaphore_signal(barrier, inc=1, device_id=other, device_id_type=MESH)

    zero_rows = jnp.zeros((K - R, W), BF16)
    loads["of"].wait()
    xg[me] = jnp.zeros((R, W), BF16)
    xg[me, 0:SEQ] = of_ref[...]
    loads["gs"].wait()
    gg[me, 0:R] = jnp.zeros((R, W), BF16)
    gg[me, 0:SEQ] = gs_ref[...]
    for b in range(4):
        gg[b, R:K] = zero_rows
        xb[b, R:K] = zero_rows
        for ref in (im, act, gh):
            ref[R:K, b * W : (b + 1) * W] = zero_rows
    for ref in (qs, ks, vs, hs):
        ref[R:K] = zero_rows
    pl.semaphore_wait(barrier, len(others))

    def gather_start(ref):
        own = ref.at[me, 0:R]
        return [net.copy(own, own, d_far), net.copy(own, own, d_sib)]

    def gather_forward(ref, two):
        two[0].wait_recv()
        got = ref.at[far, 0:R]
        two.append(net.copy(got, got, d_sib))

    def gather_end(two):
        two[1].wait_recv()
        two[2].wait_recv()

    def gain_of(ref, b):
        return ref[0:1, b * W : (b + 1) * W]

    def gain_at(ref, b):
        return ref[0:1, pl.ds(pl.multiple_of(b * W, W), W)]

    def rows_at(ref, q):
        return ref[pl.ds(pl.multiple_of(q * W, W), W), :]

    def normalize(block, gain_ref):
        total = jnp.zeros((R, 1), F32)
        for b in range(4):
            total = total + jnp.sum(block(b), 1, keepdims=True)
        mean = total * (1.0 / 1024)
        square = jnp.zeros((R, 1), F32)
        for b in range(4):
            centre = block(b) - mean
            nm[b] = centre
            square = square + jnp.sum(centre * centre, 1, keepdims=True)
        spread = lax.rsqrt(square * (1.0 / 1024) + EPS)
        for b in range(4):
            normed = nm[b] * spread
            nm[b] = normed
            im[0:R, b * W : (b + 1) * W] = (normed * gain_of(gain_ref, b)).astype(BF16)
        return spread

    def turn(lhs, block):
        for b in range(4):
            lhs[b * W : (b + 1) * W] = block(b).T

    lane = lax.broadcasted_iota(jnp.int32, (R, 128), 1)

    def stats_of(part, q, gain_ref, sums):
        scaled = part * gain_at(gain_ref, q)
        one = sums[0] + jnp.sum(scaled, 1, keepdims=True)
        two = sums[1] + jnp.sum(scaled * nm[q], 1, keepdims=True)
        return (one, two)

    def stats_send(sums, stat):
        both = jnp.where(lane == 0, sums[0], jnp.where(lane == 1, sums[1], 0.0))
        both = jnp.concatenate([both, jnp.zeros((K - R, 128), F32)], 0)
        stat[0] = both.T[0:8, :]
        triples = [(stat.at[0], stat.at[k + 1], d) for k, d in enumerate((d_sib, d_far, d_diag))]
        return net.copies(triples, stat.at[1:4])

    def stats_end(sent, stat):
        sent.wait_recv()
        total = (stat[0] + stat[1]) + (stat[2] + stat[3])
        wide = jnp.concatenate([total * (1.0 / 1024), jnp.zeros((120, K), F32)], 0).T
        return wide[0:R, 0:1], wide[0:R, 1:2]

    def norm_back(part_of, gain_ref, pair, mine, out, inn, stat, stop, between):
        phase("nb_parts")
        sums = (jnp.zeros((R, 1), F32), jnp.zeros((R, 1), F32))
        for slot, q in ((0, sib), (1, diag)):
            part = part_of(q)
            pair[0, slot] = part
            sums = stats_of(part, q, gain_ref, sums)
        swap = net.copy(pair.at[0], pair.at[1], d_sib)
        for slot, q in ((0, far), (1, me)):
            part = part_of(q)
            mine[slot] = part
            sums = stats_of(part, q, gain_ref, sums)
        sent = stats_send(sums, stat)
        phase("nb_swap_wait")
        swap.wait_recv()
        out[...] = (mine[0] + pair[1, 1]).astype(BF16)
        last = net.copy(out, inn, d_far)
        tick(*TICKS[stop])
        between()
        phase("nb_last_wait")
        last.wait_recv()
        first_mean, second_mean = stats_end(sent, stat)
        grad = mine[1] + pair[1, 0] + inn[...].astype(F32)
        return grad, first_mean, second_mean

    def outer_term(lhs, rhs, scatter, col):
        first, buf = scatter
        for b in range(4):
            tile = nn(lhs[b * W : (b + 1) * W], rhs).astype(BF16).reshape(2, 2, 4, 16, W)
            if first == "z":
                buf[2 * b : 2 * b + 2, :, :, :, col : col + W] = tile
            else:
                for x in range(4):
                    buf[x, 2 * b : 2 * b + 2, :, :, col : col + W] = tile[:, :, x]

    def writer(ref, lo, hi):
        def finish(total):
            ref[:, lo:hi] = total

        return finish

    def kind_writer(k):
        def finish(total):
            o_qkv[k] = total

        return finish

    targets = {
        "outer": lambda lo, hi: writer(o_outer, lo, hi),
        "inner": lambda lo, hi: writer(o_inner, lo, hi),
        "proj": lambda lo, hi: writer(o_proj, lo, hi),
        "q": lambda lo, hi: kind_writer(0),
        "k": lambda lo, hi: kind_writer(1),
        "v": lambda lo, hi: kind_writer(2),
    }
    scatters, at = {}, 0
    for name, what, first, lo, hi in PIECES:
        bufs = rest[at : at + 4]
        at += 4
        scatters[name] = (Scatter(net, first, bufs, targets[what](lo, hi)), (first, bufs[0]))

    def finish_small1(total):
        for n in range(4):
            o_bias[0:1, n * W : (n + 1) * W] = total[n : n + 1]
        o_gmlp[...] = total[4:5]

    def finish_small2(total):
        o_gattn[...] = total[0:1]

    small1 = Everyone(net, rest[at : at + 2], finish_small1)
    small2 = Everyone(net, rest[at + 2 : at + 4], finish_small2)

    def make(what, lhs, tile_of):
        for name, kind, first, lo, hi in PIECES:
            if kind == what:
                for col in range(lo, hi, W):
                    outer_term(lhs, tile_of(col), scatters[name][1], col - lo)
                scatters[name][0].tick()

    def tick(*names):
        for name in names:
            phase("tick_" + name)
            if name == "s1":
                small1.tick()
            elif name == "s2":
                small2.tick()
            else:
                scatters[name][0].tick()

    x_all = gather_start(xg)
    g_all = gather_start(gg)
    phase("gather_x_wait")
    gather_forward(xg, x_all)
    gather_end(x_all)
    phase("norm_mlp")
    loads["gm"].wait()
    spread_mlp = normalize(lambda b: xg[b].astype(F32), gain_mlp_ref)
    phase("hidden")
    loads["bias"].wait()
    loads["wi"].wait()
    for n in range(4):
        cols = slice(n * W, (n + 1) * W)
        u = nn(im[0:R], wi[:, cols]) + bias_ref[0:1, cols]
        square = u * u
        t = jnp.tanh(GELU_A * (u + GELU_B * (square * u)))
        half = 0.5 * (1.0 + t)
        act[0:R, cols] = (u * half).astype(BF16)
        slope = 0.5 * GELU_A * (1.0 - t * t) * (1.0 + 3.0 * GELU_B * square)
        dg[0:R, cols] = half + u * slope
        if n == 1:
            gather_forward(gg, g_all)
    phase("mlp_out")
    loads["wo"].wait()
    pair_a[0, 0] = nt(act[0:R], rows_at(wo, sib))
    pair_a[0, 1] = nt(act[0:R], rows_at(wo, diag))
    pair_mlp = net.copy(pair_a.at[0], pair_a.at[1], d_sib)
    mine_a[0] = nt(act[0:R], rows_at(wo, far))
    mine_a[1] = nt(act[0:R], rows_at(wo, me))
    phase("g_wait")
    gather_end(g_all)
    phase("turn_g")
    turn(lhs_a, lambda b: gg[b])
    phase("pair_mlp_wait")
    pair_mlp.wait_recv()
    out_a[...] = (mine_a[0] + pair_a[1, 1]).astype(BF16)
    far_mlp = net.copy(out_a, in_a, d_far)
    phase("outer_grad")
    make("outer", lhs_a, lambda col: act[:, col : col + W])

    phase("grad_active")
    bias_rows = []
    for n in range(4):
        cols = slice(n * W, (n + 1) * W)
        grad_active = nn(gg[0, 0:R], wo[0:W, cols])
        for b in range(1, 4):
            grad_active = grad_active + nn(gg[b, 0:R], wo[b * W : (b + 1) * W, cols])
        low = (grad_active * dg[0:R, cols]).astype(BF16)
        gh[0:R, cols] = low
        bias_rows.append(jnp.sum(low.astype(F32), 0, keepdims=True))

    valid = lax.broadcasted_iota(jnp.int32, (SEQ, W), 0) < SEQ
    ends = {}

    def between_mlp():
        phase("turn_im")
        turn(lhs_b, lambda b: im[:, b * W : (b + 1) * W])
        phase("far_mlp_wait")
        far_mlp.wait_recv()
        phase("input_second")
        loads["os"].wait()
        mlp = mine_a[1] + pair_a[1, 0] + in_a[...].astype(F32)
        second = (os_ref[...].astype(F32) - mlp[0:SEQ]).astype(BF16)
        o_second[...] = second
        xs[me] = jnp.zeros((R, W), BF16)
        xs[me, 0:SEQ] = second
        ends["second"] = gather_start(xs)
        phase("inner_grad")
        make("inner", lhs_b, lambda col: gh[:, col : col + W])
        tick(*TICKS["inner"])

    grad, first_mean, second_mean = norm_back(
        lambda q: nt(gh[0:R], rows_at(wi, q)),
        gain_mlp_ref, pair_b, mine_b, out_b, in_b, stat_a, "swap", between_mlp,
    )
    phase("back_first")
    loads["gf"].wait()
    normed_own = nm[me]
    back = spread_mlp * (grad * gain_at(gain_mlp_ref, me) - first_mean - normed_own * second_mean)
    first = (gf_ref[...].astype(F32) + back[0:SEQ]).astype(BF16)
    o_bfirst[...] = first
    xb[me, 0:R] = jnp.zeros((R, W), BF16)
    xb[me, 0:SEQ] = first
    b_all = gather_start(xb)
    block = bias_rows + [jnp.sum(grad * normed_own, 0, keepdims=True), jnp.zeros((3, W), F32)]
    small1.send(jnp.concatenate(block, 0))
    tick(*TICKS["back"])
    phase("xs_forward")
    gather_forward(xs, ends["second"])
    tick(*TICKS["forward"])
    phase("xs_wait")
    gather_end(ends["second"])

    phase("norm_attn")
    loads["ga"].wait()
    spread_attn = normalize(lambda b: xs[b].astype(F32), gain_attn_ref)
    phase("qkv")
    loads["wq"].wait()
    for kind, ref in enumerate((qs, ks, vs)):
        ref[0:R] = nn(im[0:R], wq[kind]).astype(BF16)
    phase("turn_attn")
    turn(lhs_a, lambda b: im[:, b * W : (b + 1) * W])
    tick(*TICKS["qkv"])

    head_lane = lax.broadcasted_iota(jnp.int32, (K, W), 1) // 64
    key_ok = lax.broadcasted_iota(jnp.int32, (K, K), 1) < SEQ
    factor = 0.125

    def only(ref, h):
        return jnp.where(head_lane == h, ref[...], jnp.zeros((), BF16))

    for h in range(4):
        phase(f"probs_{h}")
        scores = jnp.where(key_ok, nt(only(qs, h), ks[...]) * factor, -1e30)
        e = jnp.exp(scores - jnp.max(scores, 1, keepdims=True))
        probs = e / jnp.sum(e, 1, keepdims=True)
        probs_s[h] = probs
        a_h = nn(probs.astype(BF16), only(vs, h))
        if h == 0:
            rows_s[0] = a_h
        else:
            rows_s[0] += a_h
        if h == 1:
            phase("xb_forward")
            gather_forward(xb, b_all)
    tick(*TICKS["probs"])
    phase("attn_out")
    rows_low = rows_s[0].astype(BF16)
    loads["wp"].wait()
    for slot, q in ((0, sib), (1, diag)):
        pair_c[0, slot] = nt(rows_low[0:R], rows_at(wp, q))
    pair_out = net.copy(pair_c.at[0], pair_c.at[1], d_sib)
    for slot, q in ((0, far), (1, me)):
        mine_a[slot] = nt(rows_low[0:R], rows_at(wp, q))
    phase("xb_wait")
    gather_end(b_all)
    phase("grad_heads")
    heads = nn(xb[0, 0:R], wp[0:W])
    for b in range(1, 4):
        heads = heads + nn(xb[b, 0:R], wp[b * W : (b + 1) * W])
    hs[0:R] = heads.astype(BF16)
    phase("pair_out_wait")
    pair_out.wait_recv()
    out_c[...] = (mine_a[0] + pair_c[1, 1]).astype(BF16)
    far_out = net.copy(out_c, in_c, d_far)
    phase("proj_grad")
    turn(lhs_b, lambda b: xb[b])
    make("proj", lhs_b, lambda col: rows_low)
    tick(*TICKS["heads"])

    for h in range(4):
        phase(f"head_{h}")
        q_h, k_h, g_h = only(qs, h), only(ks, h), only(hs, h)
        probs = probs_s[h]
        grad_probs = nt(g_h, vs[...])
        row_dot = jnp.sum(grad_probs * probs, 1, keepdims=True)
        grad_scores = (probs * (grad_probs - row_dot)).astype(BF16)
        gv_h = nn(probs.astype(BF16).T, g_h)
        gq_h = nn(grad_scores, k_h)
        gk_h = nn(grad_scores.T, q_h)
        if h == 0:
            rows_s[1], rows_s[2], rows_s[3] = gq_h, gk_h, gv_h
        else:
            rows_s[1] += gq_h
            rows_s[2] += gk_h
            rows_s[3] += gv_h
    phase("attn_grads")
    g3[0] = (rows_s[1] * factor).astype(BF16)
    g3[1] = (rows_s[2] * factor).astype(BF16)
    g3[2] = rows_s[3].astype(BF16)
    make("v", lhs_a, lambda col: g3[2])
    make("q", lhs_a, lambda col: g3[0])
    make("k", lhs_a, lambda col: g3[1])
    tick(*TICKS["attn"])

    def qkv_part(q):
        cols = pl.ds(pl.multiple_of(q * W, W), W)
        part = nt(g3[0, 0:R], wq[0, cols, :])
        part = part + nt(g3[1, 0:R], wq[1, cols, :])
        return part + nt(g3[2, 0:R], wq[2, cols, :])

    def between_attn():
        phase("far_out_wait")
        far_out.wait_recv()
        total = mine_a[1] + pair_c[1, 0] + in_c[...].astype(F32)
        o_first[...] = (of_ref[...].astype(F32) - total[0:SEQ]).astype(BF16)
        tick(*TICKS["last"])

    grad, first_mean, second_mean = norm_back(
        qkv_part, gain_attn_ref, pair_d, mine_b, out_d, in_d, stat_b, "pair", between_attn
    )
    phase("back_second")
    normed_own = nm[me]
    small2.send(
        jnp.concatenate([jnp.sum(grad * normed_own, 0, keepdims=True), jnp.zeros((7, W), F32)], 0)
    )
    back = spread_attn * (grad * gain_at(gain_attn_ref, me) - first_mean - normed_own * second_mean)
    o_bsecond[...] = (gs_ref[...].astype(F32) + back[0:SEQ]).astype(BF16)
    tick(*TICKS["tail"])
    assert not (small1.todo or small2.todo or any(one.todo for one, _ in scatters.values()))
    phase("drain")
    assert (net.sends, net.recvs) == (SENDS, RECVS), (net.sends, net.recvs)
    net.drain()
    phase(None)


def hand_over(*refs):
    half = len(refs) // 2
    for src, dst in zip(refs[:half], refs[half:]):
        dst[...] = src[...]


def on_device(
    out_first, out_second, grad_first, grad_second, gain_attn, gain_mlp,
    qkv_weight, proj_weight, inner_weight, inner_bias, outer_weight,
):
    sds = jax.ShapeDtypeStruct
    vmem = pl.BlockSpec(memory_space=pltpu.VMEM)
    hbm = pl.BlockSpec(memory_space=pltpu.HBM)

    def v(*shape, dtype=BF16):
        return pltpu.VMEM(shape, dtype)

    def piece_bufs(first, cols):
        if first == "z":
            return [v(8, 2, 4, 16, cols), v(2, 4, 2, 4, 16, cols), v(8, 16, cols), v(16, 128)]
        bufs = [v(4, 8, 2, 16, cols), v(2, 2, 8, 2, 16, cols)]
        if first == "x":
            return bufs + [v(16, 16, cols), v(16, 128)]
        return bufs + [v(2, 4, 2, 16, cols), v(16, cols)]

    pieces = []
    for _, _, first, lo, hi in PIECES:
        pieces += piece_bufs(first, hi - lo)
    scratch = [
        *[v(SEQ, W) for _ in range(4)], v(1, 1024, dtype=F32), v(1, 1024, dtype=F32),
        v(3, 1024, W), v(1024, W), v(1024, 1024), v(1, 1024, dtype=F32), v(1024, 1024),
        pltpu.SemaphoreType.DMA((11,)),
        pltpu.SemaphoreType.DMA((SENDS,)), pltpu.SemaphoreType.DMA((RECVS,)),
        v(4, R, W), v(4, K, W), v(4, R, W), v(4, K, W), v(4, R, W, dtype=F32),
        v(K, 1024), v(K, 1024), v(R, 1024, dtype=F32), v(K, 1024), v(1024, K), v(1024, K),
        *[v(2, 2, R, W, dtype=F32) for _ in range(4)],
        *[v(2, R, W, dtype=F32) for _ in range(2)],
        *[v(R, W) for _ in range(8)],
        v(4, 8, K, dtype=F32), v(4, 8, K, dtype=F32),
        *[v(K, W) for _ in range(4)],
        v(4, K, W, dtype=F32), v(4, K, K, dtype=F32), v(3, K, W),
        *pieces,
        *[v(n, 8, W, dtype=F32) for n in (16, 4, 16, 4)],
    ]
    shapes = [
        sds((SEQ, W), BF16), sds((SEQ, W), BF16), sds((SEQ, W), BF16), sds((SEQ, W), BF16),
        sds((3, 16, W), F32), sds((16, W), F32), sds((16, 1024), F32), sds((1, 1024), F32),
        sds((16, 1024), F32), sds((1, W), F32), sds((1, W), F32),
    ]
    outs = pl.pallas_call(
        kernel,
        out_shape=[pltpu.VMEM(o.shape, o.dtype) for o in shapes],
        in_specs=[hbm] * 11,
        out_specs=[vmem] * 11,
        scratch_shapes=scratch,
        compiler_params=pltpu.CompilerParams(
            collective_id=0, has_side_effects=True, vmem_limit_bytes=56 * 1024 * 1024
        ),
        name="block_pair",
    )(
        out_first[0], out_second[0], grad_first[0], grad_second[0],
        gain_attn.reshape(1, -1), gain_mlp.reshape(1, -1),
        jnp.swapaxes(qkv_weight, 0, 1), proj_weight, inner_weight, inner_bias.reshape(1, -1), outer_weight,
    )
    outs = pl.pallas_call(
        hand_over,
        out_shape=shapes,
        in_specs=[vmem] * 11,
        out_specs=[vmem] * 11,
        compiler_params=pltpu.CompilerParams(vmem_limit_bytes=8 * 1024 * 1024),
        name="hand_over",
    )(*outs)
    return (
        outs[0][None], outs[1][None], outs[2][None], outs[3][None],
        jnp.swapaxes(outs[4], 0, 1), outs[5], outs[6], outs[7].reshape(-1), outs[8],
        outs[9].reshape(-1), outs[10].reshape(-1),
    )


def solution(mesh):
    split = Mesh(mesh.devices.reshape(NZ, 2, NX, 2, 2), AXES)
    rows = P(DP, None, TENSOR)
    return jax.shard_map(
        on_device,
        mesh=split,
        in_specs=(
            rows, rows, rows, rows, P(), P(),
            P(None, None, TENSOR), P(None, TENSOR), P(None, TENSOR), P(TENSOR), P(None, TENSOR),
        ),
        out_specs=(
            rows, rows, rows, rows,
            P(DP, None, TENSOR), P(DP, TENSOR), P(DP, TENSOR), P(TENSOR), P(DP, TENSOR),
            P(TENSOR), P(TENSOR),
        ),
        check_vma=False,
    )
```

time: 104 us -> 76 us (0.73); the launches traced: 102 us -> 75.4 us
  local copies, waits for them, and re-layouts: 15.5 us -> 0 us
  Pallas kernels: 86.1 us -> 74.7 us
    unnamed x11 -> x0, local copies, waits for them, and re-layouts: 15.5 us -> none
    pallas_call x1 -> x2, Pallas kernels: 86.1 us -> 74.7 us  [the longest x1 73.9 us: on_device(): pl.pallas_call(kernel, out_shape=[pltpu.VMEM(o.shape, o.dtype) for o in s...]
where the time goes in v2:
time: 76 us; the launch traced here: 75.4 us
  Pallas kernels  74.7 us (98%)
    pallas_call x1, Pallas kernels, on_device(): pl.pallas_call(kernel, out_shape=[pltpu.VMEM(o.shape, o.dtype) for o in s...  73.9 us

profile of v2, /device:TPU:2, one launch (start us, length us, event | category | flops | bytes accessed | tf_op | source)
XLA Modules:
  0.0 75.4 jit_solution(10786203201717719893)
XLA Ops:
  0.6 73.9 %block_pair.1 = (bf16[197,256]{1,0:T(8,128)(2,1)S(1)}, bf16[197,256]{1,0:T(8,128)(2,1)S(1)}, bf16[197,256]{1,0:T(8,128)(2,1)S(1)}, bf16[197,256]{1,0:T(8,128)(2,...) custom-call(bf16[197,256]{1,0:T(8,128)(2,1)} %bitcast.17, ...), custom_call_target="tpu_custom_call" | custom-call | tf_op jit(solution)/shard_map/block_pair/pallas_call | solution.py:744
  74.5 0.9 %hand_over.1 = (bf16[197,256]{1,0:T(8,128)(2,1)}, bf16[197,256]{1,0:T(8,128)(2,1)}, bf16[197,256]{1,0:T(8,128)(2,1)}, bf16[197,256]{1,0:T(8,128)(2,1)}, f32[3,16...) custom-call(bf16[197,256]{1,0:T(8,128)(2,1)S(1)} %get-tuple-element., ...), custom_call_target="tpu_custom_call" | custom-call | tf_op jit(solution)/shard_map/hand_over/pallas_call | solution.py:759

commit v3 on v2

--- a/solution.py
+++ b/solution.py
@@ -17,41 +17,76 @@
 K = 256
 W = 256
 NZ, NX = 8, 4
+SIZE = {"z": NZ, "x": NX, "yl": 2}
 EPS = 1e-06
 F32 = jnp.float32
 BF16 = jnp.bfloat16
 GELU_A = 0.7978845608028654
 GELU_B = 0.044715
-SENDS, RECVS = 71, 71
+SENDS, RECVS = 78, 78
+KINDS = {
+    "a": (("ring", "x"), ("swap", "yl"), ("spread", "z")),
+    "b": (("ring", "x"), ("swap", "yl"), ("ring", "z")),
+    "c": (("ring", "z"), ("swap", "yl"), ("spread", "x")),
+    "d": (("ring", "x"), ("ring", "z"), ("swap", "yl")),
+    "e": (("ring", "z"), ("spread", "x"), ("swap", "yl")),
+    "f": (("ring", "z"), ("spread", "x", "yl")),
+    "g": (("swap", "yl"), ("ring", "x"), ("spread", "z")),
+}
 PIECES = (
-    ("A1", "outer", "z", 0, 256),
-    ("A2", "outer", "z", 256, 512),
-    ("B0", "outer", "xz", 512, 1024),
-    ("A3", "inner", "z", 0, 256),
-    ("B1", "inner", "xz", 256, 1024),
-    ("a1", "v", "z", 0, 256),
-    ("a2", "proj", "z", 0, 256),
-    ("b1", "q", "x", 0, 256),
-    ("b2", "k", "x", 0, 256),
+    ("O0", "outer", "a", 0, 256),
+    ("O1", "outer", "b", 256, 512),
+    ("O2", "outer", "c", 512, 1024),
+    ("I0", "inner", "d", 0, 256),
+    ("I1", "inner", "e", 256, 768),
+    ("I2", "inner", "a", 768, 1024),
+    ("v", "v", "a", 0, 256),
+    ("proj", "proj", "f", 0, 256),
+    ("q", "q", "a", 0, 256),
+    ("k", "k", "g", 0, 256),
 )
 TICKS = {
-    "swap": ("A1", "A2"),
-    "inner": ("B0",),
-    "back": ("A1", "A2"),
-    "forward": ("A3",),
-    "qkv": ("B1",),
-    "probs": ("A1", "A2"),
-    "heads": ("A3", "s1"),
-    "attn": ("B0", "A1", "A2"),
-    "pair": ("A3", "B0"),
-    "last": ("a1", "a2", "s1", "B0", "B1"),
+    "ga": (),
+    "swap": (),
+    "inner": (
+        "O0", "O2",
+    ),
+    "back": (
+        "O1",
+    ),
+    "forward": (
+        "I0", "I1",
+    ),
+    "qkv": (
+        "I2", "O2",
+    ),
+    "probs_half": (
+        "O0",
+    ),
+    "probs": (
+        "s1",
+    ),
+    "grad_heads": (),
+    "heads": (
+        "I1", "O1",
+    ),
+    "heads_half": (
+        "O0",
+    ),
+    "attn": (
+        "O2", "I0", "proj",
+    ),
+    "pair": (
+        "I2", "s1", "O1", "I1",
+    ),
+    "last": (
+        "v", "q", "O0", "O2", "I0", "k", "proj", "O1", "v",
+    ),
     "tail": (
-        "a1", "a2", "b1", "b2", "A3", "A1", "A2", "B0", "B1",
-        "a1", "a2", "A3", "B0", "B1", "b1", "b2", "s2",
-        "B0", "B1", "a1", "a2", "s2", "B1", "b1", "b2", "B1", "a1", "a2",
+        "I1", "I0", "s1", "I2", "q", "proj", "k", "O1", "O2", "v", "I0", "I1", "q", "k", "s2", "proj", "O1",
+        "I2", "O2", "I0", "I1", "s2", "v", "O1", "I0", "proj", "q", "k",
     ),
 }
-
 
 def nn(a, b):
     return lax.dot_general(a, b, (((1,), (0,)), ((), ())), preferred_element_type=F32)
@@ -166,9 +201,13 @@
         both = self.recv.at[0, 0] if step == 1 else self.recv.at[:, step - 1]
         self.flying = self.net.copies(triples, both)
 
-    def tick(self, step):
+    def tick(self, step, finish):
         self.flying.wait_recv()
         distance = self.steps - step + 1
+        if step == self.steps and finish:
+            mine = self.chunk(self.owner(0, 0))
+            finish(mine[...].astype(F32) + self.recv[0, step - 1].astype(F32) + self.recv[1, step - 1].astype(F32))
+            return
         for way in (0, 1):
             got = self.part(self.recv.at[way, step - 1], way, distance)
             mine = self.part(self.chunk(self.owner(way, distance - 1)), way, distance)
@@ -177,102 +216,115 @@
             self.send(step + 1)
 
 
+class Swap:
+    def __init__(self, net, part, recv):
+        self.net, self.part, self.recv = net, part, recv
+        self.yl = net.pos["yl"]
+        self.steps = 1
+
+    def send(self, step):
+        target = self.net.dev(yl=1 - self.yl)
+        self.flying = self.net.copy(self.part((1 - self.yl,)), self.recv, target)
+
+    def tick(self, step, finish):
+        self.flying.wait_recv()
+        mine = self.part((self.yl,))
+        if finish:
+            finish(mine[...].astype(F32) + self.recv[...].astype(F32))
+        else:
+            add_into(mine, self.recv)
+
+
 class Spread:
-    def __init__(self, net, ring, size, recv):
-        self.net, self.ring, self.size, self.recv = net, ring, size, recv
-
-    def start(self, piece):
-        net, ring, size = self.net, self.ring, self.size
-        triples = []
-        for j in range(1, 2 * size):
-            there = lax.rem(net.pos[ring] + j % size, size)
-            y = lax.rem(net.pos["yl"] + j // size, 2)
-            triples.append((piece(there, y), self.recv.at[j], net.dev(**{ring: there, "yl": y})))
-        self.flying = net.copies(triples, self.recv.at[1 : 2 * size])
-
-    def end(self, own):
+    def __init__(self, net, axes, part, recv):
+        self.net, self.axes, self.part, self.recv = net, axes, part, recv
+        self.steps = 1
+
+    def send(self, step):
+        net, triples = self.net, []
+        count = self.recv.shape[0]
+        for j in range(1, count):
+            there, rest = {}, j
+            for axis in self.axes:
+                n = SIZE[axis]
+                there[axis] = lax.rem(net.pos[axis] + rest % n, n)
+                rest //= n
+            src = self.part(tuple(there[a] for a in self.axes))
+            triples.append((src, self.recv.at[j], net.dev(**there)))
+        self.flying = net.copies(triples, self.recv.at[1:count])
+
+    def tick(self, step, finish):
         self.flying.wait_recv()
-        total = own
-        for j in range(1, 2 * self.size):
+        mine = self.part(tuple(self.net.pos[a] for a in self.axes))
+        total = mine[...].astype(F32)
+        for j in range(1, self.recv.shape[0]):
             total = total + self.recv[j].astype(F32)
-        return total
+        if finish:
+            finish(total)
+        else:
+            mine[...] = total.astype(BF16)
 
 
 class Scatter:
-    def __init__(self, net, first, bufs, finish):
-        z, x, yl = net.pos["z"], net.pos["x"], net.pos["yl"]
-        buf = bufs[0]
-        self.todo = []
-        if first == "z":
-            one = Chain(net, lambda o: buf.at[o], "z", NZ, bufs[1])
-            last = Spread(net, "x", NX, bufs[2])
-            piece = lambda there, y: buf.at[z, y, there]
-            own = lambda: buf[z, yl, x].astype(F32)
-        else:
-            one = Chain(net, lambda o: buf.at[o], "x", NX, bufs[1])
-            piece = lambda there, y: buf.at[x, there, y]
-            own = lambda: buf[x, z, yl].astype(F32)
-            if first == "xz":
-                two = Chain(net, lambda o: buf.at[x, o], "z", NZ, bufs[2])
+    def __init__(self, net, stages, bufs, finish):
+        buf, before, steps = bufs[0], (), []
+        for k, (how, *axes) in enumerate(stages):
+            part = functools.partial(lambda before, here: buf.at[before + here], before)
+            if how == "ring":
+                chunk = functools.partial(lambda part, o: part((o,)), part)
+                stage = Chain(net, chunk, axes[0], SIZE[axes[0]], bufs[k + 1])
+            elif how == "swap":
+                stage = Swap(net, part, bufs[k + 1])
             else:
-                last = Spread(net, "z", NZ, bufs[2])
-        self.todo.append(functools.partial(one.send, 1))
-        for k in range(1, one.steps):
-            self.todo.append(functools.partial(one.tick, k))
-        if first == "xz":
-
-            def turn():
-                one.tick(one.steps)
-                two.send(1)
-
-            self.todo.append(turn)
-            for k in range(1, two.steps):
-                self.todo.append(functools.partial(two.tick, k))
-
-            def across():
-                two.tick(two.steps)
-                self.flying = net.copy(buf.at[x, z, 1 - yl], bufs[3], net.dev(yl=1 - yl))
-
-            def end():
-                self.flying.wait_recv()
-                finish(own() + bufs[3][...].astype(F32))
-
-            self.todo += [across, end]
-        else:
-
-            def turn():
-                one.tick(one.steps)
-                last.start(piece)
-
-            self.todo += [turn, lambda: finish(last.end(own()))]
+                stage = Spread(net, axes, part, bufs[k + 1])
+            before = before + tuple(net.pos[a] for a in axes)
+            steps.append(stage)
+        self.todo = [functools.partial(steps[0].send, 1)]
+        for k, stage in enumerate(steps):
+            last = k + 1 == len(steps)
+            for step in range(1, stage.steps + 1):
+                turn = last and step == stage.steps
+                follow = steps[k + 1] if not last and step == stage.steps else None
+                self.todo.append(functools.partial(self.advance, stage, step, finish if turn else None, follow))
+
+    def advance(self, stage, step, finish, follow):
+        stage.tick(step, finish)
+        if follow is not None:
+            follow.send(1)
 
     def tick(self):
         self.todo.pop(0)()
 
 
 class Everyone:
-    def __init__(self, net, slots, finish):
+    def __init__(self, net, stages, slots, finish):
         self.net, self.slots, self.finish = net, slots, finish
-        self.todo = [self.turn, self.end]
-
-    def send(self, block):
-        self.slots[0][0] = block
-        self.one = Spread(self.net, "z", NZ, self.slots[0])
-        self.one.start(lambda there, y: self.slots[0].at[0])
-
-    def turn(self):
-        net, slot = self.net, self.slots[1]
-        slot[0] = self.one.end(self.slots[0][0])
+        self.stages = stages
+        self.todo = [functools.partial(self.turn, k) for k in range(len(stages))]
+
+    def send(self, block, k=0):
+        net, slot = self.net, self.slots[k]
+        slot[0] = block
         triples = []
-        for k in range(1, NX):
-            target = net.dev(x=lax.rem(net.pos["x"] + k, NX))
-            triples.append((slot.at[0], slot.at[k], target))
-        self.flying = net.copies(triples, slot.at[1:NX])
-
-    def end(self):
+        for j in range(1, slot.shape[0]):
+            there, rest = {}, j
+            for axis in self.stages[k]:
+                n = SIZE[axis]
+                there[axis] = lax.rem(net.pos[axis] + rest % n, n)
+                rest //= n
+            triples.append((slot.at[0], slot.at[j], net.dev(**there)))
+        self.flying = net.copies(triples, slot.at[1 : slot.shape[0]])
+
+    def turn(self, k):
         self.flying.wait_recv()
-        slot = self.slots[1]
-        self.finish(((slot[0] + slot[1]) + slot[2]) + slot[3])
+        slot = self.slots[k]
+        total = slot[0]
+        for j in range(1, slot.shape[0]):
+            total = total + slot[j]
+        if k + 1 < len(self.stages):
+            self.send(total, k + 1)
+        else:
+            self.finish(total)
 
     def tick(self):
         self.todo.pop(0)()
@@ -423,14 +475,15 @@
         return grad, first_mean, second_mean
 
     def outer_term(lhs, rhs, scatter, col):
-        first, buf = scatter
+        order, buf = scatter
         for b in range(4):
             tile = nn(lhs[b * W : (b + 1) * W], rhs).astype(BF16).reshape(2, 2, 4, 16, W)
-            if first == "z":
-                buf[2 * b : 2 * b + 2, :, :, :, col : col + W] = tile
-            else:
-                for x in range(4):
-                    buf[x, 2 * b : 2 * b + 2, :, :, col : col + W] = tile[:, :, x]
+            for z in range(2):
+                for y in range(2):
+                    for x in range(4):
+                        at = {"z": 2 * b + z, "yl": y, "x": x}
+                        where = tuple(at[a] for a in order)
+                        buf[where + (slice(None), slice(col, col + W))] = tile[z, y, x]
 
     def writer(ref, lo, hi):
         def finish(total):
@@ -453,10 +506,12 @@
         "v": lambda lo, hi: kind_writer(2),
     }
     scatters, at = {}, 0
-    for name, what, first, lo, hi in PIECES:
-        bufs = rest[at : at + 4]
-        at += 4
-        scatters[name] = (Scatter(net, first, bufs, targets[what](lo, hi)), (first, bufs[0]))
+    for name, what, kind, lo, hi in PIECES:
+        stages = KINDS[kind]
+        bufs = rest[at : at + len(stages) + 1]
+        at += len(stages) + 1
+        order = [a for stage in stages for a in stage[1:]]
+        scatters[name] = (Scatter(net, stages, bufs, targets[what](lo, hi)), (order, bufs[0]))
 
     def finish_small1(total):
         for n in range(4):
@@ -464,10 +519,11 @@
         o_gmlp[...] = total[4:5]
 
     def finish_small2(total):
-        o_gattn[...] = total[0:1]
-
-    small1 = Everyone(net, rest[at : at + 2], finish_small1)
-    small2 = Everyone(net, rest[at + 2 : at + 4], finish_small2)
+        o_gattn[0:1, 0:128] = total[0:1]
+        o_gattn[0:1, 128:256] = total[1:2]
+
+    small1 = Everyone(net, (("x",), ("z",), ("yl",)), rest[at : at + 3], finish_small1)
+    small2 = Everyone(net, (("z", "yl"), ("x",)), rest[at + 3 : at + 5], finish_small2)
 
     def make(what, lhs, tile_of):
         for name, kind, first, lo, hi in PIECES:
@@ -536,6 +592,7 @@
         low = (grad_active * dg[0:R, cols]).astype(BF16)
         gh[0:R, cols] = low
         bias_rows.append(jnp.sum(low.astype(F32), 0, keepdims=True))
+    tick(*TICKS["ga"])
 
     valid = lax.broadcasted_iota(jnp.int32, (SEQ, W), 0) < SEQ
     ends = {}
@@ -611,6 +668,7 @@
         if h == 1:
             phase("xb_forward")
             gather_forward(xb, b_all)
+            tick(*TICKS["probs_half"])
     tick(*TICKS["probs"])
     phase("attn_out")
     rows_low = rows_s[0].astype(BF16)
@@ -627,6 +685,7 @@
     for b in range(1, 4):
         heads = heads + nn(xb[b, 0:R], wp[b * W : (b + 1) * W])
     hs[0:R] = heads.astype(BF16)
+    tick(*TICKS["grad_heads"])
     phase("pair_out_wait")
     pair_out.wait_recv()
     out_c[...] = (mine_a[0] + pair_c[1, 1]).astype(BF16)
@@ -652,6 +711,8 @@
             rows_s[1] += gq_h
             rows_s[2] += gk_h
             rows_s[3] += gv_h
+        if h == 1:
+            tick(*TICKS["heads_half"])
     phase("attn_grads")
     g3[0] = (rows_s[1] * factor).astype(BF16)
     g3[1] = (rows_s[2] * factor).astype(BF16)
@@ -679,8 +740,9 @@
     )
     phase("back_second")
     normed_own = nm[me]
+    gain_row = jnp.sum(grad * normed_own, 0, keepdims=True)
     small2.send(
-        jnp.concatenate([jnp.sum(grad * normed_own, 0, keepdims=True), jnp.zeros((7, W), F32)], 0)
+        jnp.concatenate([gain_row[:, 0:128], gain_row[:, 128:256], jnp.zeros((6, 128), F32)], 0)
     )
     back = spread_attn * (grad * gain_at(gain_attn_ref, me) - first_mean - normed_own * second_mean)
     o_bsecond[...] = (gs_ref[...].astype(F32) + back[0:SEQ]).astype(BF16)
@@ -709,17 +771,25 @@
     def v(*shape, dtype=BF16):
         return pltpu.VMEM(shape, dtype)
 
-    def piece_bufs(first, cols):
-        if first == "z":
-            return [v(8, 2, 4, 16, cols), v(2, 4, 2, 4, 16, cols), v(8, 16, cols), v(16, 128)]
-        bufs = [v(4, 8, 2, 16, cols), v(2, 2, 8, 2, 16, cols)]
-        if first == "x":
-            return bufs + [v(16, 16, cols), v(16, 128)]
-        return bufs + [v(2, 4, 2, 16, cols), v(16, cols)]
+    def piece_bufs(stages, cols):
+        left = [a for stage in stages for a in stage[1:]]
+        bufs = [v(*[SIZE[a] for a in left], 16, cols)]
+        for how, *axes in stages:
+            left = left[len(axes) :]
+            shape = [SIZE[a] for a in left] + [16, cols]
+            if how == "ring":
+                shape = [2, SIZE[axes[0]] // 2] + shape
+            elif how == "spread":
+                count = 1
+                for a in axes:
+                    count *= SIZE[a]
+                shape = [count] + shape
+            bufs.append(v(*shape))
+        return bufs
 
     pieces = []
-    for _, _, first, lo, hi in PIECES:
-        pieces += piece_bufs(first, hi - lo)
+    for _, _, kind, lo, hi in PIECES:
+        pieces += piece_bufs(KINDS[kind], hi - lo)
     scratch = [
         *[v(SEQ, W) for _ in range(4)], v(1, 1024, dtype=F32), v(1, 1024, dtype=F32),
         v(3, 1024, W), v(1024, W), v(1024, 1024), v(1, 1024, dtype=F32), v(1024, 1024),
@@ -734,7 +804,7 @@
         *[v(K, W) for _ in range(4)],
         v(4, K, W, dtype=F32), v(4, K, K, dtype=F32), v(3, K, W),
         *pieces,
-        *[v(n, 8, W, dtype=F32) for n in (16, 4, 16, 4)],
+        *[v(n, 8, W, dtype=F32) for n in (4, 8, 2)], *[v(n, 8, 128, dtype=F32) for n in (16, 4)],
     ]
     shapes = [
         sds((SEQ, W), BF16), sds((SEQ, W), BF16), sds((SEQ, W), BF16), sds((SEQ, W), BF16),

time: 76 us -> 68.1 us (0.90)
  Pallas kernels: 74.7 us -> 66.7 us
    pallas_call x1, Pallas kernels: 73.9 us -> 65.8 us  [on_device(): pl.pallas_call(kernel, out_shape=[pltpu.VMEM(o.shape, o.dtype) for o in s...]
where the time goes in v3:
time: 68.1 us; the launch traced here: 67.4 us
  Pallas kernels  66.7 us (98%)
    pallas_call x1, Pallas kernels, on_device(): pl.pallas_call(kernel, out_shape=[pltpu.VMEM(o.shape, o.dtype) for o in s...  65.8 us

profile of v3, /device:TPU:2, one launch (start us, length us, event | category | flops | bytes accessed | tf_op | source)
XLA Modules:
  0.0 67.4 jit_solution(9011236147239860571)
XLA Ops:
  0.6 65.8 %block_pair.1 = (bf16[197,256]{1,0:T(8,128)(2,1)S(1)}, bf16[197,256]{1,0:T(8,128)(2,1)S(1)}, bf16[197,256]{1,0:T(8,128)(2,1)S(1)}, bf16[197,256]{1,0:T(8,128)(2,...) custom-call(bf16[197,256]{1,0:T(8,128)(2,1)} %bitcast.17, ...), custom_call_target="tpu_custom_call" | custom-call | tf_op jit(solution)/shard_map/block_pair/pallas_call | solution.py:814
  66.5 0.9 %hand_over.1 = (bf16[197,256]{1,0:T(8,128)(2,1)}, bf16[197,256]{1,0:T(8,128)(2,1)}, bf16[197,256]{1,0:T(8,128)(2,1)}, bf16[197,256]{1,0:T(8,128)(2,1)}, f32[3,16...) custom-call(bf16[197,256]{1,0:T(8,128)(2,1)S(1)} %get-tuple-element., ...), custom_call_target="tpu_custom_call" | custom-call | tf_op jit(solution)/shard_map/hand_over/pallas_call | solution.py:829

commit v4 on v3

--- a/solution.py
+++ b/solution.py
@@ -23,68 +23,62 @@
 BF16 = jnp.bfloat16
 GELU_A = 0.7978845608028654
 GELU_B = 0.044715
-SENDS, RECVS = 78, 78
+ORDER = ("k", "q")
+SENDS, RECVS = 77, 77
 KINDS = {
     "a": (("ring", "x"), ("swap", "yl"), ("spread", "z")),
-    "b": (("ring", "x"), ("swap", "yl"), ("ring", "z")),
-    "c": (("ring", "z"), ("swap", "yl"), ("spread", "x")),
-    "d": (("ring", "x"), ("ring", "z"), ("swap", "yl")),
-    "e": (("ring", "z"), ("spread", "x"), ("swap", "yl")),
-    "f": (("ring", "z"), ("spread", "x", "yl")),
-    "g": (("swap", "yl"), ("ring", "x"), ("spread", "z")),
+    "b": (("ring", "z"), ("spread", "x", "yl")),
+    "c": (("ring", "x"), ("swap", "yl"), ("ring", "z")),
+    "d": (("ring", "z"), ("swap", "yl"), ("spread", "x")),
+    "e": (("swap", "yl"), ("ring", "x"), ("spread", "z")),
 }
 PIECES = (
-    ("O0", "outer", "a", 0, 256),
-    ("O1", "outer", "b", 256, 512),
-    ("O2", "outer", "c", 512, 1024),
-    ("I0", "inner", "d", 0, 256),
-    ("I1", "inner", "e", 256, 768),
-    ("I2", "inner", "a", 768, 1024),
+    ("O0", "outer0", "a", 0, 256),
+    ("O1", "outer", "b", 256, 768),
+    ("O2", "outer", "b", 768, 1024),
+    ("I0", "inner", "c", 0, 256),
+    ("I1", "inner", "d", 256, 768),
+    ("I2", "inner", "c", 768, 1024),
     ("v", "v", "a", 0, 256),
-    ("proj", "proj", "f", 0, 256),
+    ("proj", "proj", "e", 0, 256),
     ("q", "q", "a", 0, 256),
-    ("k", "k", "g", 0, 256),
+    ("k", "k", "a", 0, 256),
 )
 TICKS = {
     "ga": (),
     "swap": (),
     "inner": (
-        "O0", "O2",
+        "O0",
     ),
     "back": (
-        "O1",
+        "O1", "O2",
     ),
     "forward": (
-        "I0", "I1",
+        "I0", "I1", "I2",
     ),
-    "qkv": (
-        "I2", "O2",
-    ),
+    "qkv": (),
     "probs_half": (
         "O0",
     ),
     "probs": (
-        "s1",
+        "s1", "O1",
     ),
     "grad_heads": (),
-    "heads": (
-        "I1", "O1",
+    "heads": (),
+    "value": (
+        "O2", "I0",
     ),
-    "heads_half": (
-        "O0",
-    ),
+    "heads_half": (),
     "attn": (
-        "O2", "I0", "proj",
+        "O0", "I1", "I2",
     ),
     "pair": (
-        "I2", "s1", "O1", "I1",
-    ),
-    "last": (
-        "v", "q", "O0", "O2", "I0", "k", "proj", "O1", "v",
+        "v",
     ),
     "tail": (
-        "I1", "I0", "s1", "I2", "q", "proj", "k", "O1", "O2", "v", "I0", "I1", "q", "k", "s2", "proj", "O1",
-        "I2", "O2", "I0", "I1", "s2", "v", "O1", "I0", "proj", "q", "k",
+        "s1", "O1", "k", "O2", "proj", "q", "I0", "I2", "v", "O0", "I1", "first", "k", "O1", "proj",
+        "second", "s1", "O2", "I0", "I2", "v", "q", "k", "I1", "I0", "I2", "proj", "O1", "q", "s2", "O2",
+        "I0", "I2", "I1", "v", "k", "I0", "I2", "s2", "proj", "I1", "q",
     ),
 }
 
@@ -101,26 +95,7 @@
 
 
 def add_into(dst, src):
-    lead = dst.shape[:-2]
-    total = 1
-    for n in lead:
-        total *= n
-    if total == 1:
-        where = (0,) * len(lead)
-        dst[where] = dst[where] + src[where]
-        return
-
-    def body(j, _):
-        where = []
-        rest = j
-        for n in reversed(lead):
-            where.append(lax.rem(rest, n))
-            rest = lax.div(rest, n)
-        where = tuple(reversed(where))
-        dst[where] = dst[where] + src[where]
-        return 0
-
-    lax.fori_loop(0, total, body, 0)
+    dst[...] = dst[...] + src[...]
 
 
 class Phases:
@@ -335,7 +310,7 @@
     o_first, o_second, o_bfirst, o_bsecond, o_qkv, o_proj, o_inner, o_bias, o_outer, o_gattn, o_gmlp,
     of_ref, os_ref, gf_ref, gs_ref, gain_attn_ref, gain_mlp_ref, wq, wp, wi, bias_ref, wo,
     load_sem, send_sem, recv_sem,
-    xg, gg, xs, xb, nm, im, act, dg, gh, lhs_a, lhs_b,
+    xg, gg, xs, xb, nm, im, act, us, dg, gh, lhs_a, lhs_b,
     pair_a, pair_b, pair_c, pair_d, mine_a, mine_b, out_a, out_b, out_c, out_d, in_a, in_b, in_c, in_d,
     stat_a, stat_b, qs, ks, vs, hs, rows_s, probs_s, g3,
     *rest,
@@ -449,7 +424,7 @@
         wide = jnp.concatenate([total * (1.0 / 1024), jnp.zeros((120, K), F32)], 0).T
         return wide[0:R, 0:1], wide[0:R, 1:2]
 
-    def norm_back(part_of, gain_ref, pair, mine, out, inn, stat, stop, between):
+    def norm_back(part_of, gain_ref, pair, mine, out, inn, stat, stop, early):
         phase("nb_parts")
         sums = (jnp.zeros((R, 1), F32), jnp.zeros((R, 1), F32))
         for slot, q in ((0, sib), (1, diag)):
@@ -462,17 +437,21 @@
             mine[slot] = part
             sums = stats_of(part, q, gain_ref, sums)
         sent = stats_send(sums, stat)
+        early()
         phase("nb_swap_wait")
         swap.wait_recv()
         out[...] = (mine[0] + pair[1, 1]).astype(BF16)
         last = net.copy(out, inn, d_far)
         tick(*TICKS[stop])
-        between()
-        phase("nb_last_wait")
-        last.wait_recv()
-        first_mean, second_mean = stats_end(sent, stat)
-        grad = mine[1] + pair[1, 0] + inn[...].astype(F32)
-        return grad, first_mean, second_mean
+
+        def end():
+            phase("nb_last_wait")
+            last.wait_recv()
+            first_mean, second_mean = stats_end(sent, stat)
+            grad = mine[1] + pair[1, 0] + inn[...].astype(F32)
+            return grad, first_mean, second_mean
+
+        return end
 
     def outer_term(lhs, rhs, scatter, col):
         order, buf = scatter
@@ -499,6 +478,7 @@
 
     targets = {
         "outer": lambda lo, hi: writer(o_outer, lo, hi),
+        "outer0": lambda lo, hi: writer(o_outer, lo, hi),
         "inner": lambda lo, hi: writer(o_inner, lo, hi),
         "proj": lambda lo, hi: writer(o_proj, lo, hi),
         "q": lambda lo, hi: kind_writer(0),
@@ -523,7 +503,7 @@
         o_gattn[0:1, 128:256] = total[1:2]
 
     small1 = Everyone(net, (("x",), ("z",), ("yl",)), rest[at : at + 3], finish_small1)
-    small2 = Everyone(net, (("z", "yl"), ("x",)), rest[at + 3 : at + 5], finish_small2)
+    small2 = Everyone(net, (("z",), ("x", "yl")), rest[at + 3 : at + 5], finish_small2)
 
     def make(what, lhs, tile_of):
         for name, kind, first, lo, hi in PIECES:
@@ -560,8 +540,8 @@
         t = jnp.tanh(GELU_A * (u + GELU_B * (square * u)))
         half = 0.5 * (1.0 + t)
         act[0:R, cols] = (u * half).astype(BF16)
-        slope = 0.5 * GELU_A * (1.0 - t * t) * (1.0 + 3.0 * GELU_B * square)
-        dg[0:R, cols] = half + u * slope
+        us[:, cols] = u
+        dg[:, cols] = half
         if n == 1:
             gather_forward(gg, g_all)
     phase("mlp_out")
@@ -573,14 +553,24 @@
     mine_a[1] = nt(act[0:R], rows_at(wo, me))
     phase("g_wait")
     gather_end(g_all)
-    phase("turn_g")
+    phase("slope")
+    for n in range(4):
+        cols = slice(n * W, (n + 1) * W)
+        u, half = us[:, cols], dg[:, cols]
+        t = 2.0 * half - 1.0
+        slope = 0.5 * GELU_A * (1.0 - t * t) * (1.0 + 3.0 * GELU_B * (u * u))
+        dg[:, cols] = half + u * slope
     turn(lhs_a, lambda b: gg[b])
     phase("pair_mlp_wait")
     pair_mlp.wait_recv()
     out_a[...] = (mine_a[0] + pair_a[1, 1]).astype(BF16)
     far_mlp = net.copy(out_a, in_a, d_far)
-    phase("outer_grad")
-    make("outer", lhs_a, lambda col: act[:, col : col + W])
+    phase("outer_first")
+    make("outer0", lhs_a, lambda col: act[:, col : col + W])
+
+    def outer_grad():
+        phase("outer_grad")
+        make("outer", lhs_a, lambda col: act[:, col : col + W])
 
     phase("grad_active")
     bias_rows = []
@@ -600,6 +590,8 @@
     def between_mlp():
         phase("turn_im")
         turn(lhs_b, lambda b: im[:, b * W : (b + 1) * W])
+        phase("inner_grad")
+        make("inner", lhs_b, lambda col: gh[:, col : col + W])
         phase("far_mlp_wait")
         far_mlp.wait_recv()
         phase("input_second")
@@ -610,14 +602,14 @@
         xs[me] = jnp.zeros((R, W), BF16)
         xs[me, 0:SEQ] = second
         ends["second"] = gather_start(xs)
-        phase("inner_grad")
-        make("inner", lhs_b, lambda col: gh[:, col : col + W])
         tick(*TICKS["inner"])
 
-    grad, first_mean, second_mean = norm_back(
+    end_mlp = norm_back(
         lambda q: nt(gh[0:R], rows_at(wi, q)),
-        gain_mlp_ref, pair_b, mine_b, out_b, in_b, stat_a, "swap", between_mlp,
+        gain_mlp_ref, pair_b, mine_b, out_b, in_b, stat_a, "swap", outer_grad,
     )
+    between_mlp()
+    grad, first_mean, second_mean = end_mlp()
     phase("back_first")
     loads["gf"].wait()
     normed_own = nm[me]
@@ -670,31 +662,32 @@
             gather_forward(xb, b_all)
             tick(*TICKS["probs_half"])
     tick(*TICKS["probs"])
-    phase("attn_out")
     rows_low = rows_s[0].astype(BF16)
-    loads["wp"].wait()
-    for slot, q in ((0, sib), (1, diag)):
-        pair_c[0, slot] = nt(rows_low[0:R], rows_at(wp, q))
-    pair_out = net.copy(pair_c.at[0], pair_c.at[1], d_sib)
-    for slot, q in ((0, far), (1, me)):
-        mine_a[slot] = nt(rows_low[0:R], rows_at(wp, q))
     phase("xb_wait")
     gather_end(b_all)
     phase("grad_heads")
+    loads["wp"].wait()
     heads = nn(xb[0, 0:R], wp[0:W])
     for b in range(1, 4):
         heads = heads + nn(xb[b, 0:R], wp[b * W : (b + 1) * W])
     hs[0:R] = heads.astype(BF16)
     tick(*TICKS["grad_heads"])
-    phase("pair_out_wait")
-    pair_out.wait_recv()
-    out_c[...] = (mine_a[0] + pair_c[1, 1]).astype(BF16)
-    far_out = net.copy(out_c, in_c, d_far)
     phase("proj_grad")
     turn(lhs_b, lambda b: xb[b])
     make("proj", lhs_b, lambda col: rows_low)
     tick(*TICKS["heads"])
 
+    for h in range(4):
+        phase(f"value_{h}")
+        gv_h = nn(probs_s[h].astype(BF16).T, only(hs, h))
+        if h == 0:
+            rows_s[3] = gv_h
+        else:
+            rows_s[3] += gv_h
+    phase("v_grad")
+    g3[2] = rows_s[3].astype(BF16)
+    make("v", lhs_a, lambda col: g3[2])
+    tick(*TICKS["value"])
     for h in range(4):
         phase(f"head_{h}")
         q_h, k_h, g_h = only(qs, h), only(ks, h), only(hs, h)
@@ -702,24 +695,26 @@
         grad_probs = nt(g_h, vs[...])
         row_dot = jnp.sum(grad_probs * probs, 1, keepdims=True)
         grad_scores = (probs * (grad_probs - row_dot)).astype(BF16)
-        gv_h = nn(probs.astype(BF16).T, g_h)
         gq_h = nn(grad_scores, k_h)
         gk_h = nn(grad_scores.T, q_h)
         if h == 0:
-            rows_s[1], rows_s[2], rows_s[3] = gq_h, gk_h, gv_h
+            rows_s[1], rows_s[2] = gq_h, gk_h
         else:
             rows_s[1] += gq_h
             rows_s[2] += gk_h
-            rows_s[3] += gv_h
         if h == 1:
             tick(*TICKS["heads_half"])
     phase("attn_grads")
     g3[0] = (rows_s[1] * factor).astype(BF16)
     g3[1] = (rows_s[2] * factor).astype(BF16)
-    g3[2] = rows_s[3].astype(BF16)
-    make("v", lhs_a, lambda col: g3[2])
-    make("q", lhs_a, lambda col: g3[0])
-    make("k", lhs_a, lambda col: g3[1])
+    for name in ORDER:
+        make(name, lhs_a, lambda col: g3["qkv".index(name)])
+    phase("attn_out")
+    for slot, q in ((0, sib), (1, diag)):
+        pair_c[0, slot] = nt(rows_low[0:R], rows_at(wp, q))
+    pair_out = net.copy(pair_c.at[0], pair_c.at[1], d_sib)
+    for slot, q in ((0, far), (1, me)):
+        mine_a[slot] = nt(rows_low[0:R], rows_at(wp, q))
     tick(*TICKS["attn"])
 
     def qkv_part(q):
@@ -728,25 +723,42 @@
         part = part + nt(g3[1, 0:R], wq[1, cols, :])
         return part + nt(g3[2, 0:R], wq[2, cols, :])
 
-    def between_attn():
+    sent = {}
+
+    def attn_far():
+        phase("pair_out_wait")
+        pair_out.wait_recv()
+        out_c[...] = (mine_a[0] + pair_c[1, 1]).astype(BF16)
+        sent["out"] = net.copy(out_c, in_c, d_far)
+
+    end_attn = norm_back(
+        qkv_part, gain_attn_ref, pair_d, mine_b, out_d, in_d, stat_b, "pair", attn_far
+    )
+
+    def end_first():
         phase("far_out_wait")
-        far_out.wait_recv()
+        sent["out"].wait_recv()
         total = mine_a[1] + pair_c[1, 0] + in_c[...].astype(F32)
         o_first[...] = (of_ref[...].astype(F32) - total[0:SEQ]).astype(BF16)
-        tick(*TICKS["last"])
-
-    grad, first_mean, second_mean = norm_back(
-        qkv_part, gain_attn_ref, pair_d, mine_b, out_d, in_d, stat_b, "pair", between_attn
-    )
-    phase("back_second")
-    normed_own = nm[me]
-    gain_row = jnp.sum(grad * normed_own, 0, keepdims=True)
-    small2.send(
-        jnp.concatenate([gain_row[:, 0:128], gain_row[:, 128:256], jnp.zeros((6, 128), F32)], 0)
-    )
-    back = spread_attn * (grad * gain_at(gain_attn_ref, me) - first_mean - normed_own * second_mean)
-    o_bsecond[...] = (gs_ref[...].astype(F32) + back[0:SEQ]).astype(BF16)
-    tick(*TICKS["tail"])
+
+    def end_second():
+        grad, first_mean, second_mean = end_attn()
+        phase("back_second")
+        normed_own = nm[me]
+        gain_row = jnp.sum(grad * normed_own, 0, keepdims=True)
+        small2.send(
+            jnp.concatenate([gain_row[:, 0:128], gain_row[:, 128:256], jnp.zeros((6, 128), F32)], 0)
+        )
+        back = spread_attn * (grad * gain_at(gain_attn_ref, me) - first_mean - normed_own * second_mean)
+        o_bsecond[...] = (gs_ref[...].astype(F32) + back[0:SEQ]).astype(BF16)
+
+    for name in TICKS["tail"]:
+        if name == "first":
+            end_first()
+        elif name == "second":
+            end_second()
+        else:
+            tick(name)
     assert not (small1.todo or small2.todo or any(one.todo for one, _ in scatters.values()))
     phase("drain")
     assert (net.sends, net.recvs) == (SENDS, RECVS), (net.sends, net.recvs)
@@ -796,7 +808,7 @@
         pltpu.SemaphoreType.DMA((11,)),
         pltpu.SemaphoreType.DMA((SENDS,)), pltpu.SemaphoreType.DMA((RECVS,)),
         v(4, R, W), v(4, K, W), v(4, R, W), v(4, K, W), v(4, R, W, dtype=F32),
-        v(K, 1024), v(K, 1024), v(R, 1024, dtype=F32), v(K, 1024), v(1024, K), v(1024, K),
+        v(K, 1024), v(K, 1024), v(R, 1024, dtype=F32), v(R, 1024, dtype=F32), v(K, 1024), v(1024, K), v(1024, K),
         *[v(2, 2, R, W, dtype=F32) for _ in range(4)],
         *[v(2, R, W, dtype=F32) for _ in range(2)],
         *[v(R, W) for _ in range(8)],
@@ -804,7 +816,7 @@
         *[v(K, W) for _ in range(4)],
         v(4, K, W, dtype=F32), v(4, K, K, dtype=F32), v(3, K, W),
         *pieces,
-        *[v(n, 8, W, dtype=F32) for n in (4, 8, 2)], *[v(n, 8, 128, dtype=F32) for n in (16, 4)],
+        *[v(n, 8, W, dtype=F32) for n in (4, 8, 2)], *[v(n, 8, 128, dtype=F32) for n in (8, 8)],
     ]
     shapes = [
         sds((SEQ, W), BF16), sds((SEQ, W), BF16), sds((SEQ, W), BF16), sds((SEQ, W), BF16),

time: 68.1 us -> 66.9 us (0.982)
  Pallas kernels: 66.7 us -> 65.4 us
    pallas_call x1, Pallas kernels: 65.8 us -> 64.5 us  [on_device(): pl.pallas_call(kernel, out_shape=[pltpu.VMEM(o.shape, o.dtype) for o in s...]
where the time goes in v4:
time: 66.9 us; the launch traced here: 66 us
  Pallas kernels  65.4 us (98%)
    pallas_call x1, Pallas kernels, on_device(): pl.pallas_call(kernel, out_shape=[pltpu.VMEM(o.shape, o.dtype) for o in s...  64.5 us

profile of v4, /device:TPU:2, one launch (start us, length us, event | category | flops | bytes accessed | tf_op | source)
XLA Modules:
  0.0 66.0 jit_solution(10765664770987941938)
XLA Ops:
  0.6 64.5 %block_pair.1 = (bf16[197,256]{1,0:T(8,128)(2,1)S(1)}, bf16[197,256]{1,0:T(8,128)(2,1)S(1)}, bf16[197,256]{1,0:T(8,128)(2,1)S(1)}, bf16[197,256]{1,0:T(8,128)(2,...) custom-call(bf16[197,256]{1,0:T(8,128)(2,1)} %bitcast.17, ...), custom_call_target="tpu_custom_call" | custom-call | tf_op jit(solution)/shard_map/block_pair/pallas_call | solution.py:826
  65.1 0.9 %hand_over.1 = (bf16[197,256]{1,0:T(8,128)(2,1)}, bf16[197,256]{1,0:T(8,128)(2,1)}, bf16[197,256]{1,0:T(8,128)(2,1)}, bf16[197,256]{1,0:T(8,128)(2,1)}, f32[3,16...) custom-call(bf16[197,256]{1,0:T(8,128)(2,1)S(1)} %get-tuple-element., ...), custom_call_target="tpu_custom_call" | custom-call | tf_op jit(solution)/shard_map/hand_over/pallas_call | solution.py:841

commit v5 on v4

--- a/solution.py
+++ b/solution.py
@@ -23,62 +23,55 @@
 BF16 = jnp.bfloat16
 GELU_A = 0.7978845608028654
 GELU_B = 0.044715
-ORDER = ("k", "q")
-SENDS, RECVS = 77, 77
+ORDER = ("q", "k")
+SENDS, RECVS = 62, 62
 KINDS = {
-    "a": (("ring", "x"), ("swap", "yl"), ("spread", "z")),
+    "a": (("ring", "x"), ("swap", "yl"), ("ring", "z")),
     "b": (("ring", "z"), ("spread", "x", "yl")),
-    "c": (("ring", "x"), ("swap", "yl"), ("ring", "z")),
-    "d": (("ring", "z"), ("swap", "yl"), ("spread", "x")),
-    "e": (("swap", "yl"), ("ring", "x"), ("spread", "z")),
+    "c": (("spread", "x"), ("swap", "yl"), ("spread", "z")),
+    "d": (("ring", "x"), ("swap", "yl"), ("spread", "z")),
+    "e": (("swap", "yl"), ("spread", "x"), ("spread", "z")),
 }
 PIECES = (
-    ("O0", "outer0", "a", 0, 256),
-    ("O1", "outer", "b", 256, 768),
-    ("O2", "outer", "b", 768, 1024),
-    ("I0", "inner", "c", 0, 256),
-    ("I1", "inner", "d", 256, 768),
-    ("I2", "inner", "c", 768, 1024),
-    ("v", "v", "a", 0, 256),
+    ("O0", "outer0", "a", 0, 512),
+    ("O1", "outer", "b", 512, 1024),
+    ("I0", "inner", "b", 0, 768),
+    ("I1", "inner", "c", 768, 1024),
+    ("v", "v", "d", 0, 256),
     ("proj", "proj", "e", 0, 256),
-    ("q", "q", "a", 0, 256),
-    ("k", "k", "a", 0, 256),
+    ("q", "q", "d", 0, 256),
+    ("k", "k", "d", 0, 256),
 )
 TICKS = {
     "ga": (),
     "swap": (),
-    "inner": (
-        "O0",
-    ),
+    "inner": (),
     "back": (
-        "O1", "O2",
+        "O0", "O1",
     ),
     "forward": (
-        "I0", "I1", "I2",
+        "I0",
     ),
     "qkv": (),
     "probs_half": (
-        "O0",
+        "I1",
     ),
     "probs": (
         "s1", "O1",
     ),
     "grad_heads": (),
     "heads": (),
-    "value": (
-        "O2", "I0",
-    ),
+    "value": (),
     "heads_half": (),
     "attn": (
-        "O0", "I1", "I2",
+        "I1", "I0", "O0",
     ),
     "pair": (
         "v",
     ),
     "tail": (
-        "s1", "O1", "k", "O2", "proj", "q", "I0", "I2", "v", "O0", "I1", "first", "k", "O1", "proj",
-        "second", "s1", "O2", "I0", "I2", "v", "q", "k", "I1", "I0", "I2", "proj", "O1", "q", "s2", "O2",
-        "I0", "I2", "I1", "v", "k", "I0", "I2", "s2", "proj", "I1", "q",
+        "s1", "O1", "q", "k", "proj", "I1", "O0", "v", "I0", "q", "first", "O1", "O0", "s1", "second", "k",
+        "v", "q", "I0", "O0", "proj", "k", "s2", "O1", "O0", "v", "q", "I0", "O0", "proj", "s2", "k",
     ),
 }
 
@@ -348,16 +341,6 @@
     loads["of"].wait()
     xg[me] = jnp.zeros((R, W), BF16)
     xg[me, 0:SEQ] = of_ref[...]
-    loads["gs"].wait()
-    gg[me, 0:R] = jnp.zeros((R, W), BF16)
-    gg[me, 0:SEQ] = gs_ref[...]
-    for b in range(4):
-        gg[b, R:K] = zero_rows
-        xb[b, R:K] = zero_rows
-        for ref in (im, act, gh):
-            ref[R:K, b * W : (b + 1) * W] = zero_rows
-    for ref in (qs, ks, vs, hs):
-        ref[R:K] = zero_rows
     pl.semaphore_wait(barrier, len(others))
 
     def gather_start(ref):
@@ -523,7 +506,17 @@
                 scatters[name][0].tick()
 
     x_all = gather_start(xg)
+    loads["gs"].wait()
+    gg[me, 0:R] = jnp.zeros((R, W), BF16)
+    gg[me, 0:SEQ] = gs_ref[...]
     g_all = gather_start(gg)
+    for b in range(4):
+        gg[b, R:K] = zero_rows
+        xb[b, R:K] = zero_rows
+        for ref in (im, act, gh):
+            ref[R:K, b * W : (b + 1) * W] = zero_rows
+    for ref in (qs, ks, vs, hs):
+        ref[R:K] = zero_rows
     phase("gather_x_wait")
     gather_forward(xg, x_all)
     gather_end(x_all)

time: 66.9 us -> 66.4 us (level); the launches traced: 66 us -> 66.3 us
  no operation moved by 1% of the time
where the time goes in v5:
time: 66.4 us; the launch traced here: 66.3 us
  Pallas kernels  65.7 us (99%)
    pallas_call x1, Pallas kernels, on_device(): pl.pallas_call(kernel, out_shape=[pltpu.VMEM(o.shape, o.dtype) for o in s...  64.8 us

profile of v5, /device:TPU:2, one launch (start us, length us, event | category | flops | bytes accessed | tf_op | source)
XLA Modules:
  0.0 66.3 jit_solution(6025571905408148004)
XLA Ops:
  0.6 64.8 %block_pair.1 = (bf16[197,256]{1,0:T(8,128)(2,1)S(1)}, bf16[197,256]{1,0:T(8,128)(2,1)S(1)}, bf16[197,256]{1,0:T(8,128)(2,1)S(1)}, bf16[197,256]{1,0:T(8,128)(2,...) custom-call(bf16[197,256]{1,0:T(8,128)(2,1)} %bitcast.17, ...), custom_call_target="tpu_custom_call" | custom-call | tf_op jit(solution)/shard_map/block_pair/pallas_call | solution.py:819
  65.4 0.9 %hand_over.1 = (bf16[197,256]{1,0:T(8,128)(2,1)}, bf16[197,256]{1,0:T(8,128)(2,1)}, bf16[197,256]{1,0:T(8,128)(2,1)}, bf16[197,256]{1,0:T(8,128)(2,1)}, f32[3,16...) custom-call(bf16[197,256]{1,0:T(8,128)(2,1)S(1)} %get-tuple-element., ...), custom_call_target="tpu_custom_call" | custom-call | tf_op jit(solution)/shard_map/hand_over/pallas_call | solution.py:834

commit v6 on v5

--- a/solution.py
+++ b/solution.py
@@ -24,7 +24,7 @@
 GELU_A = 0.7978845608028654
 GELU_B = 0.044715
 ORDER = ("q", "k")
-SENDS, RECVS = 62, 62
+SENDS, RECVS = 48, 62
 KINDS = {
     "a": (("ring", "x"), ("swap", "yl"), ("ring", "z")),
     "b": (("ring", "z"), ("spread", "x", "yl")),
@@ -115,9 +115,10 @@
         where.update(other)
         return tuple(where[a] for a in AXES)
 
-    def copies(self, triples, sent, got=None):
-        k, m = self.sends, self.recvs
-        self.sends, self.recvs = k + 1, m + 1
+    def copies(self, triples, sent, got=None, share=None):
+        fresh = share is None or len(share) == 1
+        k, m = (self.sends if fresh else share[1]), self.recvs
+        self.sends, self.recvs = self.sends + fresh, m + 1
         assert self.sends <= SENDS and self.recvs <= RECVS
 
         def describe(src, dst, target):
@@ -133,11 +134,15 @@
         for triple in triples:
             describe(*triple).start()
         target = triples[0][2]
-        self.out.append(describe(sent, sent, target))
+        if fresh:
+            whole = sent if share is None else share[0]
+            self.out.append(describe(whole, whole, target))
+            if share is not None:
+                share.append(k)
         return describe(sent if got is None else got, sent if got is None else got, target)
 
-    def copy(self, src, dst, target):
-        return self.copies([(src, dst, target)], src, dst)
+    def copy(self, src, dst, target, share=None):
+        return self.copies([(src, dst, target)], src, dst, share)
 
     def drain(self):
         for c in self.out:
@@ -167,7 +172,9 @@
             dst = self.part(self.recv.at[way, step - 1], way, distance)
             triples.append((src, dst, self.net.dev(**{self.axis: self.owner(way, 1)})))
         both = self.recv.at[0, 0] if step == 1 else self.recv.at[:, step - 1]
-        self.flying = self.net.copies(triples, both)
+        if step == 2:
+            self.share = [self.recv.at[:, 1:]]
+        self.flying = self.net.copies(triples, both, None, None if step == 1 else self.share)
 
     def tick(self, step, finish):
         self.flying.wait_recv()
@@ -345,16 +352,17 @@
 
     def gather_start(ref):
         own = ref.at[me, 0:R]
-        return [net.copy(own, own, d_far), net.copy(own, own, d_sib)]
+        share = [ref.at[0:3, 0:R]]
+        return [net.copy(own, own, d_far, share), net.copy(own, own, d_sib, share), share]
 
     def gather_forward(ref, two):
         two[0].wait_recv()
         got = ref.at[far, 0:R]
-        two.append(net.copy(got, got, d_sib))
+        two.append(net.copy(got, got, d_sib, two[2]))
 
     def gather_end(two):
         two[1].wait_recv()
-        two[2].wait_recv()
+        two[3].wait_recv()
 
     def gain_of(ref, b):
         return ref[0:1, b * W : (b + 1) * W]
@@ -643,7 +651,7 @@
         phase(f"probs_{h}")
         scores = jnp.where(key_ok, nt(only(qs, h), ks[...]) * factor, -1e30)
         e = jnp.exp(scores - jnp.max(scores, 1, keepdims=True))
-        probs = e / jnp.sum(e, 1, keepdims=True)
+        probs = e * (1.0 / jnp.sum(e, 1, keepdims=True))
         probs_s[h] = probs
         a_h = nn(probs.astype(BF16), only(vs, h))
         if h == 0:

time: 66.4 us -> 66.2 us (level)
  no operation moved by 1% of the time
where the time goes in v6:
time: 66.2 us
  Pallas kernels  65.5 us (99%)
    pallas_call x1, Pallas kernels, on_device(): pl.pallas_call(kernel, out_shape=[pltpu.VMEM(o.shape, o.dtype) for o in s...  64.6 us

profile of v6, /device:TPU:2, one launch (start us, length us, event | category | flops | bytes accessed | tf_op | source)
XLA Modules:
  0.0 66.2 jit_solution(17235038883800654990)
XLA Ops:
  0.6 64.6 %block_pair.1 = (bf16[197,256]{1,0:T(8,128)(2,1)S(1)}, bf16[197,256]{1,0:T(8,128)(2,1)S(1)}, bf16[197,256]{1,0:T(8,128)(2,1)S(1)}, bf16[197,256]{1,0:T(8,128)(2,...) custom-call(bf16[197,256]{1,0:T(8,128)(2,1)} %bitcast.17, ...), custom_call_target="tpu_custom_call" | custom-call | tf_op jit(solution)/shard_map/block_pair/pallas_call | solution.py:827
  65.3 0.9 %hand_over.1 = (bf16[197,256]{1,0:T(8,128)(2,1)}, bf16[197,256]{1,0:T(8,128)(2,1)}, bf16[197,256]{1,0:T(8,128)(2,1)}, bf16[197,256]{1,0:T(8,128)(2,1)}, f32[3,16...) custom-call(bf16[197,256]{1,0:T(8,128)(2,1)S(1)} %get-tuple-element., ...), custom_call_target="tpu_custom_call" | custom-call | tf_op jit(solution)/shard_map/hand_over/pallas_call | solution.py:842
